TPU v7x, 32 devices: a whole 2x2x4 slice. The times are simulated.
32 devices in a mesh: dp: 16 (over z, y, x), vocab: 2 (over core).
Axes of the slice: x: 2, y: 2, z: 4, core: 2. Of those that a mesh axis runs over, the one named last changes fastest.
Arguments:
- hidden_states: bfloat16 [256, 3584], P('dp'), may hold values from -400 to 400
- targets: int32 [256], P('dp'), may hold values from 0 to 49151
- out_weight: bfloat16 [3584, 49152], P(None, ('dp', 'vocab')), may hold values from -5 to 5
Outputs:
- token_loss: float32 [256], P('dp')
- loss_mean: float32 [], replicated
All inputs are finite; a program needn't handle non-finite values.
Results may differ from a plain program's by a relative error of at most 0.0003.
Values may be sent and summed in bfloat16 or wider, within the bound.
No kernel may reach another device: no remote copies, remote signals or barrier semaphores. Data moves between devices by JAX's collectives and lax.ppermute only.
A program may use at most 64 MiB of HBM per device.

v0:
```python
import jax
import jax.numpy as jnp
from jax import lax
from jax.sharding import PartitionSpec as P


def shards(hidden_states, targets, out_weight):
    vocab_cols = out_weight.shape[1]
    local_tokens = hidden_states.shape[0]
    pairs = lax.axis_size("vocab")
    states, labels = (
        lax.all_gather(hidden_states, "dp", axis=0, tiled=True),
        lax.all_gather(targets, "dp", axis=0, tiled=True),
    )
    logits = jnp.dot(states, out_weight, preferred_element_type=jnp.float32)
    start = (lax.axis_index("dp") * pairs + lax.axis_index("vocab")) * vocab_cols
    columns = start + lax.broadcasted_iota(jnp.int32, logits.shape, 1)
    is_target = columns == labels[:, None]
    picked = jnp.sum(jnp.where(is_target, logits, 0.0), axis=1)
    local_top = jnp.max(logits, axis=1)
    row_top = lax.pmax(local_top, ("dp", "vocab"))
    exp_local = jnp.sum(jnp.exp(logits - row_top[:, None]), axis=1)
    exp_total, target_logit = lax.psum((exp_local, picked), ("dp", "vocab"))
    all_loss = row_top + jnp.log(exp_total) - target_logit
    token_loss = lax.dynamic_slice_in_dim(
        all_loss, lax.axis_index("dp") * local_tokens, local_tokens, 0
    )
    loss_mean = jnp.mean(all_loss)
    return (token_loss, loss_mean)


def solution(mesh):
    placed = (P("dp", None), P("dp"), P(None, ("dp", "vocab")))
    return jax.shard_map(
        shards, mesh=mesh, in_specs=placed, out_specs=(P("dp"), P()), check_vma=False
    )
```

profile of v0, /device:TPU:0, one launch (start us, length us, event | category | flops | bytes accessed | tf_op | source)
XLA Modules:
  0.0 168.6 jit_solution(12718670620491371241)
XLA Ops:
  7.2 0.0 all-gather.2.cloned.1.call-start
  7.2 0.7 all-gather.2.cloned.1.call-update
  7.9 1.2 dynamic-slice
  9.8 0.9 dynamic-update-slice
  10.7 16.2 %all-reduce = s32[256]{0:T(256)S(1)} all-reduce(s32[256]{0:T(256)S(1)} %dynamic-update-slice), channel_id=1, replica_groups=mesh['dp'=16,'vocab'=2] {'dp'}, use_global_device_ids=true, to_apply=%add | all-reduce | flops 256 | bytes 2048
  26.9 45.7 %all-gather.2.cloned.1.call-done = bf16[256,3584]{1,0:T(8,128)(2,1)} async-done(((bf16[16,3584]{1,0:T(8,128)(2,1)}), bf16[256,3584]{1,0:T(8,128)(2,1)}) %all-gather.2.cloned.1.call-update) | async-done | bytes 1835024 | tf_op jit(solution)/shard_map/all_gather | solution.py:12
  72.6 6.5 %fusion.1 = (f32[256]{0:T(256)S(1)}, f32[256,1536]{1,0:T(8,128)S(1)}) fusion(bf16[256,3584]{1,0:T(8,128)(2,1)} %all-gather.2.cloned.1.call-done, bf16[3584,1536]{1,0:T(8,128)(2,1)} %param.5), kind=kOutput, calls=%fused_computation.5 | convolution fusion | flops 2818965248 | bytes 14418944 | tf_op jit(solution)/shard_map/dot_general | solution.py:15
  79.1 38.5 %pmax.7 = f32[256]{0:T(256)S(1)} all-reduce(f32[256]{0:T(256)S(1)} %get-tuple-element.8), channel_id=1, replica_groups=mesh['dp'=16,'vocab'=2] {'dp','vocab'}, use_global_device_ids=true, to_apply=%region_1.2 | all-reduce | flops 256 | bytes 2048 | tf_op jit(solution)/shard_map/pmax | solution.py:21
  117.6 0.5 exponential_reduce_fusion
  118.1 40.7 %all-reduce.1 = (f32[256]{0:T(256)S(1)}, f32[256]{0:T(256)S(1)}) all-reduce(f32[256]{0:T(256)S(1)} %get-tuple-element.3, f32[256]{0:T(256)S(1)} %get-tuple-element.2), channel_id=1, replica_groups=mesh['dp'=16,'vocab'=2] {'dp','vocab'}, use_global_device_ids=true, to_apply=%region_5.6 | all-reduce | flops 512 | bytes 4096 | tf_op jit(solution)/shard_map/psum | solution.py:23
  158.8 0.6 fusion
  159.4 0.6 dynamic_slice.3
  (2 shorter events, 0.0 us)
Async XLA Ops:
  7.2 65.5 %all-gather.2.cloned.1.call-start = ((), (), s32[]{:S(2)}) async-start(), calls=%async_computation | async-start | bytes 1949696 | tf_op jit(solution)/shard_map/all_gather | solution.py:12
Sparse Core Ops, SparseCore 0:
  10.7 61.9 all-gather.1
where the time goes:
time: 169 us
  blocking collectives  95.4 us (56%)
  waiting for transfers between devices  46.4 us (27%)
  between operations  16.5 us (10%)
  matrix products  6.48 us (4%)
  local copies, waits for them, and re-layouts  2.68 us (2%)
    all_gather x1, waiting for transfers between devices, shards(): lax.all_gather(hidden_states, 'dp', axis=0, tiled=True)  45.7 us
    psum x1, blocking collectives, shards(): exp_total, target_logit = lax.psum((exp_local, picked), ('dp', 'vocab'))  40.7 us
    pmax x1, blocking collectives, shards(): row_top = lax.pmax(local_top, ('dp', 'vocab'))  38.5 us
    unnamed x1, blocking collectives  16.2 us
    dot_general x1, matrix products, shards(): logits = jnp.dot(states, out_weight, preferred_element_type=jnp.float32)  6.48 us
  transfers between devices with their start and end apart: 1, of which 1 were waited for; matrix products, arithmetic and copies ran while one was open for 1% of the time, Pallas kernels for 0%

commit v1 on v0

v1 whole, which is shorter than its diff:
```python
import jax
import jax.numpy as jnp
from jax import lax
from jax.sharding import PartitionSpec as P

LANES = 128
BASE = 256
DIGITS = 3


def everywhere(block, axes, count):
    copies = jnp.broadcast_to(block[None], (count,) + block.shape)
    return lax.all_to_all(copies, axes, 0, 0)


def shards(hidden_states, targets, out_weight):
    features, vocab_cols = out_weight.shape
    local_tokens = hidden_states.shape[0]
    groups, cores = lax.axis_size("dp"), lax.axis_size("vocab")
    group, core = lax.axis_index("dp"), lax.axis_index("vocab")
    share = local_tokens // cores
    tokens = groups * local_tokens

    digits = [(targets // BASE**i) % BASE for i in range(DIGITS)]
    digits = jnp.stack(digits, axis=1).astype(hidden_states.dtype)
    digits = jnp.pad(digits, ((0, 0), (0, LANES - DIGITS)))
    rows = jnp.concatenate([hidden_states, digits], axis=1)
    mine = lax.dynamic_slice_in_dim(rows, core * share, share, 0)
    mine = everywhere(mine, "dp", groups).reshape(groups * share, -1)
    swap = [(i, (i + 1) % cores) for i in range(cores)]
    other = lax.ppermute(mine, "vocab", swap)
    both = jnp.concatenate([mine, other], axis=0)
    states = both[:, :features]
    labels = both[:, features : features + DIGITS].astype(jnp.int32)
    labels = sum(labels[:, i] * BASE**i for i in range(DIGITS))

    logits = jnp.dot(states, out_weight, preferred_element_type=jnp.float32)
    start = (group * cores + core) * vocab_cols
    columns = start + lax.broadcasted_iota(jnp.int32, logits.shape, 1)
    is_target = columns == labels[:, None]
    picked = jnp.sum(jnp.where(is_target, logits, 0.0), axis=1)
    top = jnp.max(logits, axis=1)
    norm = top + jnp.log(jnp.sum(jnp.exp(logits - top[:, None]), axis=1))
    stats = jnp.stack([norm, picked])
    halves = stats.reshape(2, cores, groups * share)
    halves = jnp.where(core == 0, halves, halves[:, ::-1])
    stats = halves.reshape(2, tokens)

    stats = everywhere(stats, ("dp", "vocab"), groups * cores)
    norms = stats[:, 0]
    top = jnp.max(norms, axis=0)
    log_norm = top + jnp.log(jnp.sum(jnp.exp(norms - top), axis=0))
    loss = log_norm - jnp.sum(stats[:, 1], axis=0)
    loss = loss.reshape(cores, groups, share)
    token_loss = lax.dynamic_slice_in_dim(loss, group, 1, 1)
    return token_loss.reshape(local_tokens), jnp.sum(loss) / tokens


def solution(mesh):
    placed = (P("dp", None), P("dp"), P(None, ("dp", "vocab")))
    return jax.shard_map(
        shards, mesh=mesh, in_specs=placed, out_specs=(P("dp"), P()), check_vma=False
    )
```

time: 169 us -> 58.4 us (0.35)
  blocking collectives: 95.4 us -> 32.6 us
  waiting for transfers between devices: 46.4 us -> 9.92 us
  between operations: 16.5 us -> 2.47 us
  starting transfers between devices: 0.04 us -> 2.68 us
  other arithmetic: 1.11 us -> 2.99 us
    all_gather x1 -> x0, waiting for transfers between devices: 45.7 us -> none  [shards(): lax.all_gather(hidden_states, 'dp', axis=0, tiled=True)]
    psum x1 -> x0, blocking collectives: 40.7 us -> none  [shards(): exp_total, target_logit = lax.psum((exp_local, picked), ('dp', 'vocab'))]
    pmax x1 -> x0, blocking collectives: 38.5 us -> none  [shards(): row_top = lax.pmax(local_top, ('dp', 'vocab'))]
    all_to_all x0 -> x1, blocking collectives: none -> 32.6 us  [everywhere(): return lax.all_to_all(copies, axes, 0, 0)]
    unnamed x1 -> x0, blocking collectives: 16.2 us -> none
    all_to_all x0 -> x1, waiting for transfers between devices: none -> 7.41 us  [everywhere(): return lax.all_to_all(copies, axes, 0, 0)]
    all_to_all x0 -> x1, starting transfers between devices: none -> 2.68 us  [everywhere(): return lax.all_to_all(copies, axes, 0, 0)]
    ppermute x0 -> x1, waiting for transfers between devices: none -> 2.51 us  [shards(): other = lax.ppermute(mine, 'vocab', swap)]
  transfers between devices with their start and end apart: 1 -> 2, of which waited for: 1 -> 2; matrix products, arithmetic and copies ran while one was open for 1% -> 0% of each run, Pallas kernels for 0% -> 0%
where the time goes in v1:
time: 58.4 us; the launch traced here: 58.1 us
  blocking collectives  32.6 us (56%)
  waiting for transfers between devices  9.92 us (17%)
  matrix products  5.92 us (10%)
  other arithmetic  2.99 us (5%)
  starting transfers between devices  2.68 us (5%)
  between operations  2.47 us (4%)
  local copies, waits for them, and re-layouts  1.54 us (3%)
    all_to_all x1, blocking collectives, everywhere(): return lax.all_to_all(copies, axes, 0, 0)  32.6 us
    all_to_all x1, waiting for transfers between devices, everywhere(): return lax.all_to_all(copies, axes, 0, 0)  7.41 us
    dot_general x1, matrix products, shards(): logits = jnp.dot(states, out_weight, preferred_element_type=jnp.float32)  5.92 us
    all_to_all x1, starting transfers between devices, everywhere(): return lax.all_to_all(copies, axes, 0, 0)  2.68 us
    ppermute x1, waiting for transfers between devices, shards(): other = lax.ppermute(mine, 'vocab', swap)  2.51 us
  transfers between devices with their start and end apart: 2, of which 2 were waited for; matrix products, arithmetic and copies ran while one was open for 0% of the time, Pallas kernels for 0%

profile of v1, /device:TPU:0, one launch (start us, length us, event | category | flops | bytes accessed | tf_op | source)
XLA Modules:
  0.0 58.1 jit_solution(1020814485904580533)
XLA Ops:
  0.6 0.7 %fusion.12 = (bf16[16,1]{0,1:T(2,128)(2,1)S(1)}, bf16[16,1]{0,1:T(2,128)(2,1)S(1)}, bf16[16,1]{0,1:T(2,128)(2,1)S(1)}) fusion(s32[16]{0:T(128)} %param.4), kind=kLoop, calls=%fused_computation.45 | loop fusion | flops 864 | bytes 160 | tf_op jit(solution)/shard_map/stack | solution.py:25
  1.3 0.1 copy.16
  1.4 0.8 %fusion.8 = bf16[8,3712]{1,0:T(8,128)(2,1)S(1)} fusion(s32[]{:T(128)S(6)} %select_n.48, bf16[16,3584]{1,0:T(8,128)(2,1)} %param.3, bf16[16,3]{1,0:T(8,128)(2,1)S(1)} %copy.16), kind=kLoop, calls=%fused_computation.17 | loop fusion | flops 178176 | bytes 174180 | tf_op jit(solution)/shard_map/concatenate | solution.py:27
  2.3 0.1 broadcast_in_dim.10
  2.3 32.6 %all_to_all.10 = bf16[16,8,3712]{2,1,0:T(8,128)(2,1)S(1)} all-to-all(bf16[16,8,3712]{2,1,0:T(8,128)(2,1)S(1)} %broadcast_in_dim.10), channel_id=1, replica_groups=mesh['dp'=16,'vocab'=2] {'dp'}, dimensions={0} | all-to-all | bytes 1900544 | tf_op jit(solution)/shard_map/all_to_all | solution.py:13
  34.9 0.0 collective-permute-start
  34.9 2.5 %collective-permute-done = bf16[128,3712]{1,0:T(8,128)(2,1)S(1)} collective-permute-done((bf16[128,3712]{1,0:T(8,128)(2,1)S(1)}, bf16[128,3712]{1,0:T(8,128)(2,1)S(1)}, u32[]{:S(2)}, u32[]{:S(2)}) %collective-permute-start) | collective-permute-done | bytes 950304 | tf_op jit(solution)/shard_map/ppermute | solution.py:31
  37.5 0.2 fusion.4
  37.7 5.9 %fusion.21 = (f32[256]{0:T(256)S(1)}, f32[256,1536]{1,0:T(8,128)S(1)}) fusion(bf16[3584,1536]{1,0:T(8,128)(2,1)} %param.5, bf16[128,3712]{1,0:T(8,128)(2,1)S(1)} %bitcast.24, bf16[128,3712]{1,0:T(8,128)(2,1)S(1)} %collective-permute-done), kind=kOutput, calls=%fused_computation.56 | convolution fusion | flops 2822635264 | bytes 14484480 | tf_op jit(solution)/shard_map/dot_general | solution.py:37
  43.6 0.5 exponential_reduce_fusion
  44.2 0.6 %broadcast_in_dim.23 = f32[32,2,256]{2,1,0:T(2,128)} broadcast(f32[2,256]{1,0:T(2,128)S(1)} %bitcast.27), dimensions={1,2} | broadcast | bytes 67584 | tf_op jit(solution)/shard_map/broadcast_in_dim | solution.py:12
  44.8 2.7 %all-to-all-start.1 = ((f32[32,2,256]{2,1,0:T(2,128)}), f32[32,2,256]{2,1,0:T(2,128)S(1)}, u32[]{:S(2)}, u32[]{:S(2)}) async-start(f32[32,2,256]{2,1,0:T(2,128)} %broadcast_in_dim.23), calls=%async_computation.1 | async-start | bytes 131072 | tf_op jit(solution)/shard_map/all_to_all | solution.py:13
  47.5 7.4 %all-to-all-done.1 = f32[32,2,256]{2,1,0:T(2,128)S(1)} async-done(((f32[32,2,256]{2,1,0:T(2,128)}), f32[32,2,256]{2,1,0:T(2,128)S(1)}, u32[]{:S(2)}, u32[]{:S(2)}) %all-to-all-start.1) | async-done | bytes 65568 | tf_op jit(solution)/shard_map/all_to_all | solution.py:13
  54.9 0.1 slice_reduce_fusion.1
  55.0 0.6 %fusion.20 = (f32[]{:T(128)}, f32[256]{0:T(256)S(1)}) fusion(f32[256]{0:T(256)S(1)} %get-tuple-element.5, f32[256]{0:T(256)S(1)} %get-tuple-element.4, f32[256]{0:T(256)S(1)} %fusion.10), kind=kLoop, calls=%fused_computation.55 | loop fusion | flops 767 | bytes 4100 | tf_op jit(solution)/shard_map/reduce_sum | solution.py:56
  55.6 0.1 sub.39
  55.7 0.6 %reshape.50 = f32[16]{0:T(128)} reshape(f32[2,8]{1,0:T(2,128)S(1)} %dynamic-slice_reduce_fusion) | data formatting | bytes 128 | tf_op jit(solution)/shard_map/reshape | solution.py:56
  (10 shorter events, 0.1 us)
Async XLA Ops:
  34.9 2.5 %collective-permute-start = (bf16[128,3712]{1,0:T(8,128)(2,1)S(1)}, bf16[128,3712]{1,0:T(8,128)(2,1)S(1)}, u32[]{:S(2)}, u32[]{:S(2)}) collective-permute-start(bf16[128,3712]{1,0:T(8,128)(2,1)S(1)} %bitcast.22), channel_id=1, source_target_pairs={{0,1},{1,0},{2,3},{3,2},{4,5},{5,4},{6,7},{7,6},{8,9},{9,8},{10,11... | collective-permute-start | bytes 2850824 | tf_op jit(solution)/shard_map/ppermute | solution.py:31
  44.8 10.1 %all-to-all-start.1 = ((f32[32,2,256]{2,1,0:T(2,128)}), f32[32,2,256]{2,1,0:T(2,128)S(1)}, u32[]{:S(2)}, u32[]{:S(2)}) async-start(f32[32,2,256]{2,1,0:T(2,128)} %broadcast_in_dim.23), calls=%async_computation.1 | async-start | bytes 131072 | tf_op jit(solution)/shard_map/all_to_all | solution.py:13

commit v2 on v0

v2 whole, which is shorter than its diff:
```python
import functools

import jax
import jax.numpy as jnp
from jax import lax
from jax.experimental import pallas as pl
from jax.experimental.pallas import tpu as pltpu
from jax.sharding import PartitionSpec as P

LANES = 128
SUB = 8
BASE = 256
DIGITS = 3
TILE = 256
VMEM = pl.BlockSpec(memory_space=pltpu.VMEM)
LIMIT = pltpu.CompilerParams(vmem_limit_bytes=20 * 2**20)
HBM = pl.BlockSpec(memory_space=pltpu.HBM)
CHUNKS = 8


def near(array):
    return pltpu.with_memory_space_constraint(array, pltpu.VMEM)


def far(array):
    return pltpu.with_memory_space_constraint(array, pltpu.HBM)


def orders(groups):
    bits = [1 << b for b in reversed(range(groups.bit_length() - 1))]
    return (bits[:-2] + bits[-1:] + bits[-2:-1], bits)


def place(order, j):
    where = 0
    for b, k in enumerate(order):
        where ^= k * ((j >> b) & 1)
    return where


def pack_kernel(share, targets_hbm, states_hbm, *refs):
    piece_refs, (targets_ref, states_ref, sems) = refs[:-3], refs[-3:]
    core = lax.axis_index("vocab")
    first = pl.multiple_of(core * share, share)
    copies = (
        pltpu.make_async_copy(targets_hbm, targets_ref, sems.at[0]),
        pltpu.make_async_copy(
            states_hbm.at[pl.ds(first, share), :], states_ref, sems.at[1]
        ),
    )
    for copy in copies:
        copy.start()
    for copy in copies:
        copy.wait()
    block = states_ref[...]
    row = lax.broadcasted_iota(jnp.int32, (share, LANES), 0)
    lane = lax.broadcasted_iota(jnp.int32, (share, LANES), 1)
    label = jnp.zeros((share, LANES), jnp.int32)
    for t in range(share):
        label = jnp.where(row == t, targets_ref[first + t], label)
    digits = jnp.zeros((share, LANES), jnp.int32)
    for d in range(DIGITS):
        digits = jnp.where(lane == d, (label >> (8 * d)) & (BASE - 1), digits)
    digits = digits.astype(jnp.float32).astype(block.dtype)
    at = 0
    for c, ref in enumerate(piece_refs):
        last = c == len(piece_refs) - 1
        width = ref.shape[1] - (LANES if last else 0)
        ref[:, :width] = block[:, at : at + width]
        at += width
        if last:
            ref[:, width:] = digits


def load_kernel(source, piece_ref, target, again_ref, sems):
    rows = source.shape[0] // CHUNKS
    copies = []
    for n in range(CHUNKS):
        part = pl.ds(n * rows, rows)
        copies.append(
            pltpu.make_async_copy(source.at[part], target.at[part], sems.at[n])
        )
        copies[-1].start()
    again_ref[...] = piece_ref[...]
    for copy in copies:
        copy.wait()


def score_kernel(plan, flip, *refs):
    pieces, rest = refs[: 2 * len(plan)], list(refs[2 * len(plan) :])
    weight_ref = rest.pop(0)
    before_ref = rest.pop(0) if flip else None
    out_ref, rows_ref, logits_ref, stats_ref = rest
    features, vocab_cols = weight_ref.shape
    rows = rows_ref.shape[0]
    group, core = lax.axis_index("dp"), lax.axis_index("vocab")
    cores = lax.axis_size("vocab")
    at = 0
    for c, order in enumerate(plan):
        early, late = pieces[2 * c : 2 * c + 2]
        width = early.shape[1]
        for j in range(rows // SUB):
            to = place(order, j) * SUB
            ref = early if j < rows // SUB // 2 else late
            at_row = j * SUB % (rows // 2)
            rows_ref[to : to + SUB, at : at + width] = ref[at_row : at_row + SUB, :]
        at += width
    states = rows_ref[:, :features]

    def multiply(n, top):
        columns = pl.ds(pl.multiple_of(n * TILE, TILE), TILE)
        part = jnp.dot(
            states, weight_ref[:, columns], preferred_element_type=jnp.float32
        )
        logits_ref[:, columns] = part
        for k in range(TILE // LANES):
            top = jnp.maximum(top, part[:, k * LANES : (k + 1) * LANES])
        return top

    top = jnp.full((rows, LANES), -jnp.inf, jnp.float32)
    top = lax.fori_loop(0, vocab_cols // TILE, multiply, top)
    top = jnp.max(top, axis=1, keepdims=True)
    digits = rows_ref[:, features:].astype(jnp.float32)
    lane = lax.broadcasted_iota(jnp.int32, (rows, LANES), 1)
    scale = jnp.where(lane == 0, 1.0, jnp.where(lane == 1, 256.0, 65536.0))
    scale = jnp.where(lane < DIGITS, scale, 0.0)
    label = jnp.sum(digits * scale, axis=1, keepdims=True).astype(jnp.int32)
    start = (group * cores + core) * vocab_cols
    offset = lane + start - label

    total = jnp.zeros((rows, LANES), jnp.float32)
    picked = jnp.zeros((rows, LANES), jnp.float32)
    for n in range(vocab_cols // LANES):
        part = logits_ref[:, n * LANES : (n + 1) * LANES]
        total = total + jnp.exp(part - top)
        picked = picked + jnp.where(offset == -n * LANES, part, 0.0)
    norm = top + jnp.log(jnp.sum(total, axis=1, keepdims=True))
    picked = jnp.sum(picked, axis=1, keepdims=True)
    stats = jnp.where(lane == 0, norm, jnp.where(lane == 1, picked, 0.0))
    for j in range(rows // SUB):
        to = pl.multiple_of((group ^ j) * SUB, SUB)
        stats_ref[pl.ds(to, SUB), :] = stats[j * SUB : (j + 1) * SUB, :]
    stats = stats_ref[...].T[:2, :]
    if not flip:
        out_ref[...] = stats
        return
    before = before_ref[...]
    low = jnp.where(core == 0, before, stats)
    high = jnp.where(core == 0, stats, before)
    out_ref[:, 0:1, :] = jnp.broadcast_to(low[0:1][None], (out_ref.shape[0], 1, rows))
    out_ref[:, 1:2, :] = jnp.broadcast_to(high[0:1][None], (out_ref.shape[0], 1, rows))
    out_ref[:, 2:3, :] = jnp.broadcast_to(low[1:2][None], (out_ref.shape[0], 1, rows))
    out_ref[:, 3:4, :] = jnp.broadcast_to(high[1:2][None], (out_ref.shape[0], 1, rows))


def finish_kernel(share, stats_ref, token_ref, mean_ref):
    group = lax.axis_index("dp")
    stats = stats_ref[...]
    length = stats.shape[-1]
    top = jnp.max(stats, axis=0)
    total = jnp.sum(jnp.exp(stats - top[None]), axis=0)
    log_norm = top + jnp.log(total)
    picked = jnp.sum(stats, axis=0)
    loss = log_norm[0:2] - picked[2:4]
    mean_ref[...] = jnp.sum(loss, keepdims=True) / (2 * length)
    lane = lax.broadcasted_iota(jnp.int32, (1, length), 1)
    low = pltpu.roll(loss[0:1], (length - group * share) % length, 1)
    high = pltpu.roll(loss[1:2], (length + share - group * share) % length, 1)
    token_ref[...] = jnp.where(lane < share, low, high)[:, : 2 * share]


def shards(hidden_states, targets, out_weight):
    features, vocab_cols = out_weight.shape
    local_tokens = hidden_states.shape[0]
    groups, cores = lax.axis_size("dp"), lax.axis_size("vocab")
    share = local_tokens // cores
    half = groups * share
    dtype = hidden_states.dtype
    plan = orders(groups)
    cut = features // len(plan) // LANES * LANES
    widths = [cut] * (len(plan) - 1)
    widths.append(features - sum(widths) + LANES)

    pieces = pl.pallas_call(
        functools.partial(pack_kernel, share),
        out_shape=[jax.ShapeDtypeStruct((share, w), dtype) for w in widths],
        in_specs=[HBM, HBM],
        out_specs=[VMEM] * len(widths),
        scratch_shapes=[
            pltpu.SMEM((local_tokens,), jnp.int32),
            pltpu.VMEM((share, features), dtype),
            pltpu.SemaphoreType.DMA((2,)),
        ],
        compiler_params=LIMIT,
        name="pack",
    )(far(targets), far(hidden_states))

    weight, again = pl.pallas_call(
        load_kernel,
        out_shape=[
            jax.ShapeDtypeStruct(out_weight.shape, dtype),
            jax.ShapeDtypeStruct(pieces[0].shape, dtype),
        ],
        in_specs=[HBM, VMEM],
        out_specs=[VMEM, VMEM],
        scratch_shapes=[pltpu.SemaphoreType.DMA((CHUNKS,))],
        compiler_params=LIMIT,
        cost_estimate=pl.CostEstimate(
            flops=2 * half * features * vocab_cols, bytes_accessed=0, transcendentals=0
        ),
        name="load",
    )(far(out_weight), pieces[0])

    mine = [[piece] for piece in pieces]
    for step in range(len(plan[0])):
        for c, order in enumerate(plan):
            flips = [(i, i ^ order[step]) for i in range(groups)]
            whole = jnp.concatenate(mine[c], axis=0)
            mine[c] = [whole, lax.ppermute(whole, "dp", flips)]
            if step == 0 and c == 0:
                mine[c][0] = again
    mine = [part for pair in mine for part in pair]
    swap = [(i, (i + 1) % cores) for i in range(cores)]
    other = [lax.ppermute(part, "vocab", swap) for part in mine]

    weight = near(weight)
    cost = pl.CostEstimate(
        flops=2 * half * features * vocab_cols,
        bytes_accessed=2 * half * features,
        transcendentals=half * vocab_cols,
    )

    def score(pieces, before):
        flip = before is not None
        shape = (groups * cores, 4, half) if flip else (2, half)
        extra = [before] if flip else []
        return pl.pallas_call(
            functools.partial(score_kernel, plan, flip),
            out_shape=jax.ShapeDtypeStruct(shape, jnp.float32),
            in_specs=[VMEM] * (len(pieces) + 1 + len(extra)),
            out_specs=VMEM,
            scratch_shapes=[
                pltpu.VMEM((half, features + LANES), dtype),
                pltpu.VMEM((half, vocab_cols), jnp.float32),
                pltpu.VMEM((half, LANES), jnp.float32),
            ],
            cost_estimate=cost,
            compiler_params=LIMIT,
            name="score_other" if flip else "score_mine",
        )(*[near(p) for p in pieces], weight, *extra)

    stats = score(other, score(mine, None))
    stats = lax.all_to_all(stats, ("dp", "vocab"), 0, 0)
    token_loss, loss_mean = pl.pallas_call(
        functools.partial(finish_kernel, share),
        out_shape=[
            jax.ShapeDtypeStruct((1, local_tokens), jnp.float32),
            jax.ShapeDtypeStruct((1, 1), jnp.float32),
        ],
        in_specs=[VMEM],
        out_specs=[VMEM, VMEM],
        compiler_params=LIMIT,
        name="finish",
    )(stats)
    return token_loss.reshape(local_tokens), loss_mean.reshape(())


def solution(mesh):
    placed = (P("dp", None), P("dp"), P(None, ("dp", "vocab")))
    return jax.shard_map(
        shards, mesh=mesh, in_specs=placed, out_specs=(P("dp"), P()), check_vma=False
    )
```

time: 169 us -> 48 us (0.28)
  blocking collectives: 95.4 us -> 12.1 us
  waiting for transfers between devices: 46.4 us -> 10.1 us
  between operations: 16.5 us -> 0.71 us
  starting transfers between devices: 0.04 us -> 12.9 us
  Pallas kernels: 0 us -> 11.9 us
  matrix products: 6.48 us -> 0 us
  local copies, waits for them, and re-layouts: 2.68 us -> 0.06 us
    all_gather x1 -> x0, waiting for transfers between devices: 45.7 us -> none  [shards(): lax.all_gather(hidden_states, 'dp', axis=0, tiled=True)]
    psum x1 -> x0, blocking collectives: 40.7 us -> none  [shards(): exp_total, target_logit = lax.psum((exp_local, picked), ('dp', 'vocab'))]
    pmax x1 -> x0, blocking collectives: 38.5 us -> none  [shards(): row_top = lax.pmax(local_top, ('dp', 'vocab'))]
    unnamed x1 -> x0, blocking collectives: 16.2 us -> none
    ppermute x0 -> x12, starting transfers between devices: none -> 12.9 us  [the longest x8 12.4 us: shards(): mine[c] = [whole, lax.ppermute(whole, 'dp', flips)]]
    all_to_all x0 -> x1, blocking collectives: none -> 12.1 us  [shards(): stats = lax.all_to_all(stats, ('dp', 'vocab'), 0, 0)]
    pallas_call x0 -> x5, Pallas kernels: none -> 11.9 us  [the longest x2 6.1 us: score(): pl.pallas_call(functools.partial(score_kernel, plan, flip), out_shape=jax...]
    ppermute x0 -> x12, waiting for transfers between devices: none -> 10.1 us  [the longest x8 10.1 us: shards(): mine[c] = [whole, lax.ppermute(whole, 'dp', flips)]]
  transfers between devices with their start and end apart: 1 -> 12, of which waited for: 1 -> 5; matrix products, arithmetic and copies ran while one was open for 1% -> 0% of each run, Pallas kernels for 0% -> 15%
where the time goes in v2:
time: 48 us; the launch traced here: 47.9 us
  starting transfers between devices  12.9 us (27%)
  blocking collectives  12.1 us (25%)
  Pallas kernels  11.9 us (25%)
  waiting for transfers between devices  10.1 us (21%)
  between operations  0.71 us (1%)
    ppermute x8, starting transfers between devices, shards(): mine[c] = [whole, lax.ppermute(whole, 'dp', flips)]  12.4 us
    all_to_all x1, blocking collectives, shards(): stats = lax.all_to_all(stats, ('dp', 'vocab'), 0, 0)  12.1 us
    ppermute x8, waiting for transfers between devices, shards(): mine[c] = [whole, lax.ppermute(whole, 'dp', flips)]  10.1 us
    pallas_call x2, Pallas kernels, score(): pl.pallas_call(functools.partial(score_kernel, plan, flip), out_shape=jax...  6.1 us
    pallas_call x1, Pallas kernels, shards(): pl.pallas_call(load_kernel, out_shape=[jax.ShapeDtypeStruct(out_weight.sh...  4.24 us
  transfers between devices with their start and end apart: 12, of which 5 were waited for; matrix products, arithmetic and copies ran while one was open for 0% of the time, Pallas kernels for 15%

profile of v2, /device:TPU:0, one launch (start us, length us, event | category | flops | bytes accessed | tf_op | source)
XLA Modules:
  0.0 47.9 jit_solution(5819895593826805890)
XLA Ops:
  0.6 0.9 %pack.1 = (bf16[8,1792]{1,0:T(8,128)(2,1)S(1)}, bf16[8,1920]{1,0:T(8,128)(2,1)S(1)}) custom-call(s32[16]{0:T(128)} %targets_hbm.1, bf16[16,3584]{1,0:T(8,128)(2,1)} %states_hbm.1), custom_call_target="tpu_custom_call" | custom-call | tf_op jit(solution)/shard_map/pack/pallas_call | solution.py:184
  1.5 4.1 %collective-permute-start.6 = (bf16[8,1920]{1,0:T(8,128)(2,1)S(1)}, bf16[8,1920]{1,0:T(8,128)(2,1)S(1)}, u32[]{:S(2)}, u32[]{:S(2)}) collective-permute-start(bf16[8,1920]{1,0:T(8,128)(2,1)S(1)} %get-tuple-element.10), channel_id=1, source_target_pairs={{0,16},{2,18},{4,20},{6,22},{8,24},{10,26},{12,28},{14,30},{16,0},... | collective-permute-start | bytes 92168 | tf_op jit(solution)/shard_map/ppermute | solution.py:219
  5.6 0.1 collective-permute-start
  5.7 4.2 %load.1 = (bf16[3584,1536]{1,0:T(8,128)(2,1)S(1)}, bf16[8,1792]{1,0:T(8,128)(2,1)S(1)}) custom-call(bf16[3584,1536]{1,0:T(8,128)(2,1)} %source.1, bf16[8,1792]{1,0:T(8,128)(2,1)S(1)} %get-tuple-element.8.piece_ref), custom_call_target="tpu_custom_call" | custom-call | flops 1409286144 | tf_op jit(solution)/shard_map/load/pallas_call | solution.py:198
  10.0 0.4 collective-permute-done
  10.4 1.6 %collective-permute-start.1 = (bf16[16,1792]{1,0:T(8,128)(2,1)S(1)}, bf16[16,1792]{1,0:T(8,128)(2,1)S(1)}, u32[]{:S(2)}, u32[]{:S(2)}) collective-permute-start(bf16[16,1792]{1,0:T(8,128)(2,1)S(1)} %pad_maximum_fusion.3), channel_id=1, source_target_pairs={{0,8},{2,10},{4,12},{6,14},{8,0},{10,2},{12,4},{14,6},{16,24},{18,... | collective-permute-start | bytes 172040 | tf_op jit(solution)/shard_map/ppermute | solution.py:219
  12.0 0.0 collective-permute-done.6
  12.0 0.5 %collective-permute-start.7 = (bf16[16,1920]{1,0:T(8,128)(2,1)S(1)}, bf16[16,1920]{1,0:T(8,128)(2,1)S(1)}, u32[]{:S(2)}, u32[]{:S(2)}) collective-permute-start(bf16[16,1920]{1,0:T(8,128)(2,1)S(1)} %pad_maximum_fusion.2), channel_id=1, source_target_pairs={{0,8},{2,10},{4,12},{6,14},{8,0},{10,2},{12,4},{14,6},{16,24},{18,... | collective-permute-start | bytes 184328 | tf_op jit(solution)/shard_map/ppermute | solution.py:219
  12.5 2.3 %collective-permute-done.1 = bf16[16,1792]{1,0:T(8,128)(2,1)S(1)} collective-permute-done((bf16[16,1792]{1,0:T(8,128)(2,1)S(1)}, bf16[16,1792]{1,0:T(8,128)(2,1)S(1)}, u32[]{:S(2)}, u32[]{:S(2)}) %collective-permute-start.1) | collective-permute-done | bytes 57376 | tf_op jit(solution)/shard_map/ppermute | solution.py:219
  14.9 1.6 %collective-permute-start.2 = (bf16[32,1792]{1,0:T(8,128)(2,1)S(1)}, bf16[32,1792]{1,0:T(8,128)(2,1)S(1)}, u32[]{:S(2)}, u32[]{:S(2)}) collective-permute-start(bf16[32,1792]{1,0:T(8,128)(2,1)S(1)} %pad_maximum_fusion.1), channel_id=1, source_target_pairs={{0,2},{2,0},{4,6},{6,4},{8,10},{10,8},{12,14},{14,12},{16,18},{18,... | collective-permute-start | bytes 344072 | tf_op jit(solution)/shard_map/ppermute | solution.py:219
  16.4 0.0 collective-permute-done.7
  16.5 1.6 %collective-permute-start.8 = (bf16[32,1920]{1,0:T(8,128)(2,1)S(1)}, bf16[32,1920]{1,0:T(8,128)(2,1)S(1)}, u32[]{:S(2)}, u32[]{:S(2)}) collective-permute-start(bf16[32,1920]{1,0:T(8,128)(2,1)S(1)} %pad_maximum_fusion), channel_id=1, source_target_pairs={{0,4},{2,6},{4,0},{6,2},{8,12},{10,14},{12,8},{14,10},{16,20},{18,... | collective-permute-start | bytes 368648 | tf_op jit(solution)/shard_map/ppermute | solution.py:219
  18.1 3.3 %collective-permute-done.8 = bf16[32,1920]{1,0:T(8,128)(2,1)S(1)} collective-permute-done((bf16[32,1920]{1,0:T(8,128)(2,1)S(1)}, bf16[32,1920]{1,0:T(8,128)(2,1)S(1)}, u32[]{:S(2)}, u32[]{:S(2)}) %collective-permute-start.8) | collective-permute-done | bytes 122912 | tf_op jit(solution)/shard_map/ppermute | solution.py:219
  21.4 1.4 %collective-permute-start.10 = (bf16[64,1920]{1,0:T(8,128)(2,1)S(1)}, bf16[64,1920]{1,0:T(8,128)(2,1)S(1)}, u32[]{:S(2)}, u32[]{:S(2)}) collective-permute-start(bf16[64,1920]{1,0:T(8,128)(2,1)S(1)} %constant_dynamic-update-slice_fusion.4.refs_2_), channel_id=1, source_target_pairs={{0,2},{2,0},{4,6},{6,4},{8,10},{10,8},{12,14},{14,12},{16,18},{18,... | collective-permute-start | bytes 737288 | tf_op jit(solution)/shard_map/ppermute | solution.py:219
  22.8 0.0 collective-permute-done.2
  22.8 1.6 %collective-permute-start.4 = (bf16[64,1792]{1,0:T(8,128)(2,1)S(1)}, bf16[64,1792]{1,0:T(8,128)(2,1)S(1)}, u32[]{:S(2)}, u32[]{:S(2)}) collective-permute-start(bf16[64,1792]{1,0:T(8,128)(2,1)S(1)} %constant_dynamic-update-slice_fusion.refs_0_), channel_id=1, source_target_pairs={{0,4},{2,6},{4,0},{6,2},{8,12},{10,14},{12,8},{14,10},{16,20},{18,... | collective-permute-start | bytes 688136 | tf_op jit(solution)/shard_map/ppermute | solution.py:219
  24.4 0.0 collective-permute-start.9
  24.4 3.3 %collective-permute-done.10.refs_3_ = bf16[64,1920]{1,0:T(8,128)(2,1)S(1)} collective-permute-done((bf16[64,1920]{1,0:T(8,128)(2,1)S(1)}, bf16[64,1920]{1,0:T(8,128)(2,1)S(1)}, u32[]{:S(2)}, u32[]{:S(2)}) %collective-permute-start.10) | collective-permute-done | bytes 245792 | tf_op jit(solution)/shard_map/ppermute | solution.py:219
  27.7 0.0 collective-permute-start.11
  27.7 0.5 %collective-permute-start.3 = (bf16[64,1792]{1,0:T(8,128)(2,1)S(1)}, bf16[64,1792]{1,0:T(8,128)(2,1)S(1)}, u32[]{:S(2)}, u32[]{:S(2)}) collective-permute-start(bf16[64,1792]{1,0:T(8,128)(2,1)S(1)} %constant_dynamic-update-slice_fusion.refs_0_), channel_id=1, source_target_pairs={{0,1},{1,0},{2,3},{3,2},{4,5},{5,4},{6,7},{7,6},{8,9},{9,8},{10,11... | collective-permute-start | bytes 688136 | tf_op jit(solution)/shard_map/ppermute | solution.py:224
  28.2 0.7 %collective-permute-done.4.refs_1_ = bf16[64,1792]{1,0:T(8,128)(2,1)S(1)} collective-permute-done((bf16[64,1792]{1,0:T(8,128)(2,1)S(1)}, bf16[64,1792]{1,0:T(8,128)(2,1)S(1)}, u32[]{:S(2)}, u32[]{:S(2)}) %collective-permute-start.4) | collective-permute-done | bytes 229408 | tf_op jit(solution)/shard_map/ppermute | solution.py:219
  28.9 0.0 collective-permute-start.5
  28.9 3.0 %score_mine.1.refs_5_ = f32[2,128]{1,0:T(2,128)S(1)} custom-call(bf16[64,1792]{1,0:T(8,128)(2,1)S(1)} %constant_dynamic-update-slice_fusion.refs_0_, bf16[64,1792]{1,0:T(8,128)(2,1)S(1)} %collective-permute-done.4.refs_1_, bf16[64,1920]{1,0:T(8,128)(2,1)S(1)} %constant_dynamic-update-slice_fusion.4.refs_2_, ...), custom_call_target="tpu_custom_call" | custom-call | flops 1409286144 | bytes 917504 | tf_op jit(solution)/shard_map/score_mine/pallas_call | solution.py:237
  32.0 0.0 collective-permute-done.3.refs_0_
  32.0 0.0 collective-permute-done.9.refs_2_
  32.0 0.0 collective-permute-done.5.refs_1_
  32.0 0.0 collective-permute-done.11.refs_3_
  32.0 3.1 %score_other.1 = f32[32,4,128]{2,1,0:T(4,128)S(1)} custom-call(bf16[64,1792]{1,0:T(8,128)(2,1)S(1)} %collective-permute-done.3.refs_0_, bf16[64,1792]{1,0:T(8,128)(2,1)S(1)} %collective-permute-done.5.refs_1_, bf16[64,1920]{1,0:T(8,128)(2,1)S(1)} %collective-permute-done.9.refs_2_, bf16[64,1920]{1,0:T(8,128)(2,1)S(1)} %collective-permute-done.11.refs_3_, ...), custom_call_target="tpu_custom_call" | custom-call | flops 1409286144 | bytes 917504 | tf_op jit(solution)/shard_map/score_other/pallas_call | solution.py:237
  35.1 12.1 %all_to_all.5.stats_ref = f32[32,4,128]{2,1,0:T(4,128)S(1)} all-to-all(f32[32,4,128]{2,1,0:T(4,128)S(1)} %score_other.1), channel_id=1, replica_groups=mesh['dp'=16,'vocab'=2] {'dp','vocab'}, dimensions={0} | all-to-all | bytes 131072 | tf_op jit(solution)/shard_map/all_to_all | solution.py:253
  47.2 0.7 %finish.1 = (f32[1,16]{1,0:T(1,128)}, f32[1,1]{1,0:T(1,128)}) custom-call(f32[32,4,128]{2,1,0:T(4,128)S(1)} %all_to_all.5.stats_ref), custom_call_target="tpu_custom_call" | custom-call | tf_op jit(solution)/shard_map/finish/pallas_call | solution.py:254
  (12 shorter events, 0.1 us)
Async XLA Ops:
  1.5 10.5 %collective-permute-start.6 = (bf16[8,1920]{1,0:T(8,128)(2,1)S(1)}, bf16[8,1920]{1,0:T(8,128)(2,1)S(1)}, u32[]{:S(2)}, u32[]{:S(2)}) collective-permute-start(bf16[8,1920]{1,0:T(8,128)(2,1)S(1)} %get-tuple-element.10), channel_id=1, source_target_pairs={{0,16},{2,18},{4,20},{6,22},{8,24},{10,26},{12,28},{14,30},{16,0},... | collective-permute-start | bytes 92168 | tf_op jit(solution)/shard_map/ppermute | solution.py:219
  5.6 4.8 %collective-permute-start = (bf16[8,1792]{1,0:T(8,128)(2,1)S(1)}, bf16[8,1792]{1,0:T(8,128)(2,1)S(1)}, u32[]{:S(2)}, u32[]{:S(2)}) collective-permute-start(bf16[8,1792]{1,0:T(8,128)(2,1)S(1)} %get-tuple-element.8.piece_ref), channel_id=1, source_target_pairs={{0,16},{2,18},{4,20},{6,22},{8,24},{10,26},{12,28},{14,30},{16,0},... | collective-permute-start | bytes 86024 | tf_op jit(solution)/shard_map/ppermute | solution.py:219
  10.4 4.5 %collective-permute-start.1 = (bf16[16,1792]{1,0:T(8,128)(2,1)S(1)}, bf16[16,1792]{1,0:T(8,128)(2,1)S(1)}, u32[]{:S(2)}, u32[]{:S(2)}) collective-permute-start(bf16[16,1792]{1,0:T(8,128)(2,1)S(1)} %pad_maximum_fusion.3), channel_id=1, source_target_pairs={{0,8},{2,10},{4,12},{6,14},{8,0},{10,2},{12,4},{14,6},{16,24},{18,... | collective-permute-start | bytes 172040 | tf_op jit(solution)/shard_map/ppermute | solution.py:219
  12.0 4.4 %collective-permute-start.7 = (bf16[16,1920]{1,0:T(8,128)(2,1)S(1)}, bf16[16,1920]{1,0:T(8,128)(2,1)S(1)}, u32[]{:S(2)}, u32[]{:S(2)}) collective-permute-start(bf16[16,1920]{1,0:T(8,128)(2,1)S(1)} %pad_maximum_fusion.2), channel_id=1, source_target_pairs={{0,8},{2,10},{4,12},{6,14},{8,0},{10,2},{12,4},{14,6},{16,24},{18,... | collective-permute-start | bytes 184328 | tf_op jit(solution)/shard_map/ppermute | solution.py:219
  14.9 7.9 %collective-permute-start.2 = (bf16[32,1792]{1,0:T(8,128)(2,1)S(1)}, bf16[32,1792]{1,0:T(8,128)(2,1)S(1)}, u32[]{:S(2)}, u32[]{:S(2)}) collective-permute-start(bf16[32,1792]{1,0:T(8,128)(2,1)S(1)} %pad_maximum_fusion.1), channel_id=1, source_target_pairs={{0,2},{2,0},{4,6},{6,4},{8,10},{10,8},{12,14},{14,12},{16,18},{18,... | collective-permute-start | bytes 344072 | tf_op jit(solution)/shard_map/ppermute | solution.py:219
  16.5 4.9 %collective-permute-start.8 = (bf16[32,1920]{1,0:T(8,128)(2,1)S(1)}, bf16[32,1920]{1,0:T(8,128)(2,1)S(1)}, u32[]{:S(2)}, u32[]{:S(2)}) collective-permute-start(bf16[32,1920]{1,0:T(8,128)(2,1)S(1)} %pad_maximum_fusion), channel_id=1, source_target_pairs={{0,4},{2,6},{4,0},{6,2},{8,12},{10,14},{12,8},{14,10},{16,20},{18,... | collective-permute-start | bytes 368648 | tf_op jit(solution)/shard_map/ppermute | solution.py:219
  21.4 6.3 %collective-permute-start.10 = (bf16[64,1920]{1,0:T(8,128)(2,1)S(1)}, bf16[64,1920]{1,0:T(8,128)(2,1)S(1)}, u32[]{:S(2)}, u32[]{:S(2)}) collective-permute-start(bf16[64,1920]{1,0:T(8,128)(2,1)S(1)} %constant_dynamic-update-slice_fusion.4.refs_2_), channel_id=1, source_target_pairs={{0,2},{2,0},{4,6},{6,4},{8,10},{10,8},{12,14},{14,12},{16,18},{18,... | collective-permute-start | bytes 737288 | tf_op jit(solution)/shard_map/ppermute | solution.py:219
  22.8 6.1 %collective-permute-start.4 = (bf16[64,1792]{1,0:T(8,128)(2,1)S(1)}, bf16[64,1792]{1,0:T(8,128)(2,1)S(1)}, u32[]{:S(2)}, u32[]{:S(2)}) collective-permute-start(bf16[64,1792]{1,0:T(8,128)(2,1)S(1)} %constant_dynamic-update-slice_fusion.refs_0_), channel_id=1, source_target_pairs={{0,4},{2,6},{4,0},{6,2},{8,12},{10,14},{12,8},{14,10},{16,20},{18,... | collective-permute-start | bytes 688136 | tf_op jit(solution)/shard_map/ppermute | solution.py:219
  24.4 7.6 %collective-permute-start.9 = (bf16[64,1920]{1,0:T(8,128)(2,1)S(1)}, bf16[64,1920]{1,0:T(8,128)(2,1)S(1)}, u32[]{:S(2)}, u32[]{:S(2)}) collective-permute-start(bf16[64,1920]{1,0:T(8,128)(2,1)S(1)} %constant_dynamic-update-slice_fusion.4.refs_2_), channel_id=1, source_target_pairs={{0,1},{1,0},{2,3},{3,2},{4,5},{5,4},{6,7},{7,6},{8,9},{9,8},{10,11... | collective-permute-start | bytes 737288 | tf_op jit(solution)/shard_map/ppermute | solution.py:224
  27.7 4.3 %collective-permute-start.11 = (bf16[64,1920]{1,0:T(8,128)(2,1)S(1)}, bf16[64,1920]{1,0:T(8,128)(2,1)S(1)}, u32[]{:S(2)}, u32[]{:S(2)}) collective-permute-start(bf16[64,1920]{1,0:T(8,128)(2,1)S(1)} %collective-permute-done.10.refs_3_), channel_id=1, source_target_pairs={{0,1},{1,0},{2,3},{3,2},{4,5},{5,4},{6,7},{7,6},{8,9},{9,8},{10,11... | collective-permute-start | bytes 737288 | tf_op jit(solution)/shard_map/ppermute | solution.py:224
  27.7 4.3 %collective-permute-start.3 = (bf16[64,1792]{1,0:T(8,128)(2,1)S(1)}, bf16[64,1792]{1,0:T(8,128)(2,1)S(1)}, u32[]{:S(2)}, u32[]{:S(2)}) collective-permute-start(bf16[64,1792]{1,0:T(8,128)(2,1)S(1)} %constant_dynamic-update-slice_fusion.refs_0_), channel_id=1, source_target_pairs={{0,1},{1,0},{2,3},{3,2},{4,5},{5,4},{6,7},{7,6},{8,9},{9,8},{10,11... | collective-permute-start | bytes 688136 | tf_op jit(solution)/shard_map/ppermute | solution.py:224
  28.9 3.1 %collective-permute-start.5 = (bf16[64,1792]{1,0:T(8,128)(2,1)S(1)}, bf16[64,1792]{1,0:T(8,128)(2,1)S(1)}, u32[]{:S(2)}, u32[]{:S(2)}) collective-permute-start(bf16[64,1792]{1,0:T(8,128)(2,1)S(1)} %collective-permute-done.4.refs_1_), channel_id=1, source_target_pairs={{0,1},{1,0},{2,3},{3,2},{4,5},{5,4},{6,7},{7,6},{8,9},{9,8},{10,11... | collective-permute-start | bytes 688136 | tf_op jit(solution)/shard_map/ppermute | solution.py:224

commit v3 on v2

--- a/solution.py
+++ b/solution.py
@@ -11,6 +11,7 @@
 SUB = 8
 BASE = 256
 DIGITS = 3
+LOADS = (2, 1)
 TILE = 256
 VMEM = pl.BlockSpec(memory_space=pltpu.VMEM)
 LIMIT = pltpu.CompilerParams(vmem_limit_bytes=20 * 2**20)
@@ -28,7 +29,7 @@
 
 def orders(groups):
     bits = [1 << b for b in reversed(range(groups.bit_length() - 1))]
-    return (bits[:-2] + bits[-1:] + bits[-2:-1], bits)
+    return (bits, bits[-1:] + bits[:-1])
 
 
 def place(order, j):
@@ -72,18 +73,42 @@
             ref[:, width:] = digits
 
 
-def load_kernel(source, piece_ref, target, again_ref, sems):
-    rows = source.shape[0] // CHUNKS
+def load_kernel(part, source, piece_ref, *refs):
+    target, again_ref, sems = refs[-3:]
+    first, size = part
+    rows = size // CHUNKS
     copies = []
     for n in range(CHUNKS):
-        part = pl.ds(n * rows, rows)
+        span = pl.ds(first + n * rows, rows)
         copies.append(
-            pltpu.make_async_copy(source.at[part], target.at[part], sems.at[n])
+            pltpu.make_async_copy(source.at[span], target.at[span], sems.at[n])
         )
         copies[-1].start()
     again_ref[...] = piece_ref[...]
     for copy in copies:
         copy.wait()
+
+
+def load(part, source, piece, target):
+    first = target is None
+    return pl.pallas_call(
+        functools.partial(load_kernel, part),
+        out_shape=[
+            jax.ShapeDtypeStruct(source.shape, source.dtype),
+            jax.ShapeDtypeStruct(piece.shape, piece.dtype),
+        ],
+        in_specs=[HBM, VMEM] + ([] if first else [VMEM]),
+        out_specs=[VMEM, VMEM],
+        scratch_shapes=[pltpu.SemaphoreType.DMA((CHUNKS,))],
+        input_output_aliases={} if first else {2: 0},
+        compiler_params=LIMIT,
+        cost_estimate=pl.CostEstimate(
+            flops=2 * part[1] * source.shape[1] * 2 * LANES,
+            bytes_accessed=0,
+            transcendentals=0,
+        ),
+        name=f"load_{part[0]}",
+    )(far(source), piece, *([] if first else [near(target)]))
 
 
 def score_kernel(plan, flip, *refs):
@@ -118,7 +143,7 @@
         return top
 
     top = jnp.full((rows, LANES), -jnp.inf, jnp.float32)
-    top = lax.fori_loop(0, vocab_cols // TILE, multiply, top)
+    top = lax.fori_loop(0, vocab_cols // TILE, multiply, top, unroll=True)
     top = jnp.max(top, axis=1, keepdims=True)
     digits = rows_ref[:, features:].astype(jnp.float32)
     lane = lax.broadcasted_iota(jnp.int32, (rows, LANES), 1)
@@ -195,30 +220,20 @@
         name="pack",
     )(far(targets), far(hidden_states))
 
-    weight, again = pl.pallas_call(
-        load_kernel,
-        out_shape=[
-            jax.ShapeDtypeStruct(out_weight.shape, dtype),
-            jax.ShapeDtypeStruct(pieces[0].shape, dtype),
-        ],
-        in_specs=[HBM, VMEM],
-        out_specs=[VMEM, VMEM],
-        scratch_shapes=[pltpu.SemaphoreType.DMA((CHUNKS,))],
-        compiler_params=LIMIT,
-        cost_estimate=pl.CostEstimate(
-            flops=2 * half * features * vocab_cols, bytes_accessed=0, transcendentals=0
-        ),
-        name="load",
-    )(far(out_weight), pieces[0])
-
+    steps = len(plan[0])
+    weight = None
     mine = [[piece] for piece in pieces]
-    for step in range(len(plan[0])):
+    done = 0
+    for step in range(steps):
         for c, order in enumerate(plan):
             flips = [(i, i ^ order[step]) for i in range(groups)]
             whole = jnp.concatenate(mine[c], axis=0)
             mine[c] = [whole, lax.ppermute(whole, "dp", flips)]
-            if step == 0 and c == 0:
-                mine[c][0] = again
+        if step < len(LOADS):
+            size = int((features - done) / LOADS[step])
+            size = size // (SUB * CHUNKS) * SUB * CHUNKS
+            weight, mine[-1][0] = load((done, size), out_weight, whole, weight)
+            done += size
     mine = [part for pair in mine for part in pair]
     swap = [(i, (i + 1) % cores) for i in range(cores)]
     other = [lax.ppermute(part, "vocab", swap) for part in mine]

time: 48 us -> 44.1 us (0.919)
  blocking collectives: 12.1 us -> 9.16 us
  Pallas kernels: 11.9 us -> 10.9 us
    all_to_all x1, blocking collectives: 12.1 us -> 9.16 us  [shards(): stats = lax.all_to_all(stats, ('dp', 'vocab'), 0, 0)]
    pallas_call x2, Pallas kernels: 6.1 us -> 4.12 us  [score(): pl.pallas_call(functools.partial(score_kernel, plan, flip), out_shape=jax...]
    pallas_call x1 -> x2, Pallas kernels: 4.24 us -> 5.24 us  [load(): pl.pallas_call(functools.partial(load_kernel, part), out_shape=[jax.Shape...]
  transfers between devices with their start and end apart: 12 -> 12, of which waited for: 5 -> 4; matrix products, arithmetic and copies ran while one was open for 0% -> 0% of each run, Pallas kernels for 15% -> 17%
where the time goes in v3:
time: 44.1 us; the launch traced here: 43.9 us
  starting transfers between devices  12.6 us (29%)
  Pallas kernels  10.9 us (25%)
  waiting for transfers between devices  10.4 us (24%)
  blocking collectives  9.16 us (21%)
  between operations  0.74 us (2%)
    ppermute x8, starting transfers between devices, shards(): mine[c] = [whole, lax.ppermute(whole, 'dp', flips)]  12.1 us
    ppermute x8, waiting for transfers between devices, shards(): mine[c] = [whole, lax.ppermute(whole, 'dp', flips)]  10.4 us
    all_to_all x1, blocking collectives, shards(): stats = lax.all_to_all(stats, ('dp', 'vocab'), 0, 0)  9.16 us
    pallas_call x2, Pallas kernels, load(): pl.pallas_call(functools.partial(load_kernel, part), out_shape=[jax.Shape...  5.24 us
    pallas_call x2, Pallas kernels, score(): pl.pallas_call(functools.partial(score_kernel, plan, flip), out_shape=jax...  4.12 us
  transfers between devices with their start and end apart: 12, of which 4 were waited for; matrix products, arithmetic and copies ran while one was open for 0% of the time, Pallas kernels for 17%

profile of v3, /device:TPU:0, one launch (start us, length us, event | category | flops | bytes accessed | tf_op | source)
XLA Modules:
  0.0 43.9 jit_solution(9799915257462595601)
XLA Ops:
  0.6 0.9 %pack.1 = (bf16[8,1792]{1,0:T(8,128)(2,1)S(1)}, bf16[8,1920]{1,0:T(8,128)(2,1)S(1)}) custom-call(s32[16]{0:T(128)} %targets_hbm.1, bf16[16,3584]{1,0:T(8,128)(2,1)} %states_hbm.1), custom_call_target="tpu_custom_call" | custom-call | tf_op jit(solution)/shard_map/pack/pallas_call | solution.py:209
  1.5 4.1 %collective-permute-start = (bf16[8,1792]{1,0:T(8,128)(2,1)S(1)}, bf16[8,1792]{1,0:T(8,128)(2,1)S(1)}, u32[]{:S(2)}, u32[]{:S(2)}) collective-permute-start(bf16[8,1792]{1,0:T(8,128)(2,1)S(1)} %get-tuple-element.10), channel_id=1, source_target_pairs={{0,16},{2,18},{4,20},{6,22},{8,24},{10,26},{12,28},{14,30},{16,0},... | collective-permute-start | bytes 86024 | tf_op jit(solution)/shard_map/ppermute | solution.py:231
  5.6 1.5 %collective-permute-start.6 = (bf16[8,1920]{1,0:T(8,128)(2,1)S(1)}, bf16[8,1920]{1,0:T(8,128)(2,1)S(1)}, u32[]{:S(2)}, u32[]{:S(2)}) collective-permute-start(bf16[8,1920]{1,0:T(8,128)(2,1)S(1)} %get-tuple-element.11.piece_ref), channel_id=1, source_target_pairs={{0,2},{2,0},{4,6},{6,4},{8,10},{10,8},{12,14},{14,12},{16,18},{18,... | collective-permute-start | bytes 92168 | tf_op jit(solution)/shard_map/ppermute | solution.py:231
  7.1 2.6 %load_0.1 = (bf16[3584,1536]{1,0:T(8,128)(2,1)S(1)}, bf16[8,1920]{1,0:T(8,128)(2,1)S(1)}) custom-call(bf16[3584,1536]{1,0:T(8,128)(2,1)} %source.3, bf16[8,1920]{1,0:T(8,128)(2,1)S(1)} %get-tuple-element.11.piece_ref), custom_call_target="tpu_custom_call" | custom-call | flops 1409286144 | tf_op jit(solution)/shard_map/load_0/pallas_call | solution.py:94
  9.8 0.0 collective-permute-done
  9.8 1.6 %collective-permute-start.1 = (bf16[16,1792]{1,0:T(8,128)(2,1)S(1)}, bf16[16,1792]{1,0:T(8,128)(2,1)S(1)}, u32[]{:S(2)}, u32[]{:S(2)}) collective-permute-start(bf16[16,1792]{1,0:T(8,128)(2,1)S(1)} %pad_maximum_fusion.2), channel_id=1, source_target_pairs={{0,8},{2,10},{4,12},{6,14},{8,0},{10,2},{12,4},{14,6},{16,24},{18,... | collective-permute-start | bytes 172040 | tf_op jit(solution)/shard_map/ppermute | solution.py:231
  11.4 0.0 collective-permute-done.6
  11.4 0.8 %collective-permute-start.7 = (bf16[16,1920]{1,0:T(8,128)(2,1)S(1)}, bf16[16,1920]{1,0:T(8,128)(2,1)S(1)}, u32[]{:S(2)}, u32[]{:S(2)}) collective-permute-start(bf16[16,1920]{1,0:T(8,128)(2,1)S(1)} %constant_dynamic-update-slice_fusion.4.piece_ref), channel_id=1, source_target_pairs={{0,16},{2,18},{4,20},{6,22},{8,24},{10,26},{12,28},{14,30},{16,0},... | collective-permute-start | bytes 184328 | tf_op jit(solution)/shard_map/ppermute | solution.py:231
  12.3 2.6 %load_1792.1 = (bf16[3584,1536]{1,0:T(8,128)(2,1)S(1)}, bf16[16,1920]{1,0:T(8,128)(2,1)S(1)}) custom-call(bf16[3584,1536]{1,0:T(8,128)(2,1)} %source.3, bf16[16,1920]{1,0:T(8,128)(2,1)S(1)} %constant_dynamic-update-slice_fusion.4.piece_ref, bf16[3584,1536]{1,0:T(8,128)(2,1)S(1)} %get-tuple-element.13.refs_0_), custom_call_target="tpu_custom_call", output_to_operand_aliasing={{0}: (2, {})} | custom-call | flops 1409286144 | tf_op jit(solution)/shard_map/load_1792/pallas_call | solution.py:94
  14.9 0.0 collective-permute-done.1
  14.9 1.6 %collective-permute-start.2 = (bf16[32,1792]{1,0:T(8,128)(2,1)S(1)}, bf16[32,1792]{1,0:T(8,128)(2,1)S(1)}, u32[]{:S(2)}, u32[]{:S(2)}) collective-permute-start(bf16[32,1792]{1,0:T(8,128)(2,1)S(1)} %pad_maximum_fusion.1), channel_id=1, source_target_pairs={{0,4},{2,6},{4,0},{6,2},{8,12},{10,14},{12,8},{14,10},{16,20},{18,... | collective-permute-start | bytes 344072 | tf_op jit(solution)/shard_map/ppermute | solution.py:231
  16.5 0.7 %collective-permute-done.7 = bf16[16,1920]{1,0:T(8,128)(2,1)S(1)} collective-permute-done((bf16[16,1920]{1,0:T(8,128)(2,1)S(1)}, bf16[16,1920]{1,0:T(8,128)(2,1)S(1)}, u32[]{:S(2)}, u32[]{:S(2)}) %collective-permute-start.7) | collective-permute-done | bytes 61472 | tf_op jit(solution)/shard_map/ppermute | solution.py:231
  17.2 0.1 collective-permute-start.8
  17.3 4.8 %collective-permute-done.8 = bf16[32,1920]{1,0:T(8,128)(2,1)S(1)} collective-permute-done((bf16[32,1920]{1,0:T(8,128)(2,1)S(1)}, bf16[32,1920]{1,0:T(8,128)(2,1)S(1)}, u32[]{:S(2)}, u32[]{:S(2)}) %collective-permute-start.8) | collective-permute-done | bytes 122912 | tf_op jit(solution)/shard_map/ppermute | solution.py:231
  22.1 1.6 %collective-permute-start.10 = (bf16[64,1920]{1,0:T(8,128)(2,1)S(1)}, bf16[64,1920]{1,0:T(8,128)(2,1)S(1)}, u32[]{:S(2)}, u32[]{:S(2)}) collective-permute-start(bf16[64,1920]{1,0:T(8,128)(2,1)S(1)} %constant_dynamic-update-slice_fusion.6.refs_2_), channel_id=1, source_target_pairs={{0,4},{2,6},{4,0},{6,2},{8,12},{10,14},{12,8},{14,10},{16,20},{18,... | collective-permute-start | bytes 737288 | tf_op jit(solution)/shard_map/ppermute | solution.py:231
  23.7 0.0 collective-permute-done.2
  23.8 0.7 %collective-permute-start.4 = (bf16[64,1792]{1,0:T(8,128)(2,1)S(1)}, bf16[64,1792]{1,0:T(8,128)(2,1)S(1)}, u32[]{:S(2)}, u32[]{:S(2)}) collective-permute-start(bf16[64,1792]{1,0:T(8,128)(2,1)S(1)} %constant_dynamic-update-slice_fusion.refs_0_), channel_id=1, source_target_pairs={{0,2},{2,0},{4,6},{6,4},{8,10},{10,8},{12,14},{14,12},{16,18},{18,... | collective-permute-start | bytes 688136 | tf_op jit(solution)/shard_map/ppermute | solution.py:231
  24.5 0.0 collective-permute-start.9
  24.5 4.0 %collective-permute-done.10.refs_3_ = bf16[64,1920]{1,0:T(8,128)(2,1)S(1)} collective-permute-done((bf16[64,1920]{1,0:T(8,128)(2,1)S(1)}, bf16[64,1920]{1,0:T(8,128)(2,1)S(1)}, u32[]{:S(2)}, u32[]{:S(2)}) %collective-permute-start.10) | collective-permute-done | bytes 245792 | tf_op jit(solution)/shard_map/ppermute | solution.py:231
  28.4 0.0 collective-permute-start.11
  28.4 0.5 %collective-permute-start.3 = (bf16[64,1792]{1,0:T(8,128)(2,1)S(1)}, bf16[64,1792]{1,0:T(8,128)(2,1)S(1)}, u32[]{:S(2)}, u32[]{:S(2)}) collective-permute-start(bf16[64,1792]{1,0:T(8,128)(2,1)S(1)} %constant_dynamic-update-slice_fusion.refs_0_), channel_id=1, source_target_pairs={{0,1},{1,0},{2,3},{3,2},{4,5},{5,4},{6,7},{7,6},{8,9},{9,8},{10,11... | collective-permute-start | bytes 688136 | tf_op jit(solution)/shard_map/ppermute | solution.py:239
  28.9 0.9 %collective-permute-done.4.refs_1_ = bf16[64,1792]{1,0:T(8,128)(2,1)S(1)} collective-permute-done((bf16[64,1792]{1,0:T(8,128)(2,1)S(1)}, bf16[64,1792]{1,0:T(8,128)(2,1)S(1)}, u32[]{:S(2)}, u32[]{:S(2)}) %collective-permute-start.4) | collective-permute-done | bytes 229408 | tf_op jit(solution)/shard_map/ppermute | solution.py:231
  29.8 0.0 collective-permute-start.5
  29.8 2.0 %score_mine.1.refs_5_ = f32[2,128]{1,0:T(2,128)S(1)} custom-call(bf16[64,1792]{1,0:T(8,128)(2,1)S(1)} %constant_dynamic-update-slice_fusion.refs_0_, bf16[64,1792]{1,0:T(8,128)(2,1)S(1)} %collective-permute-done.4.refs_1_, bf16[64,1920]{1,0:T(8,128)(2,1)S(1)} %constant_dynamic-update-slice_fusion.6.refs_2_, ...), custom_call_target="tpu_custom_call" | custom-call | flops 1409286144 | bytes 917504 | tf_op jit(solution)/shard_map/score_mine/pallas_call | solution.py:252
  31.9 0.0 collective-permute-done.3.refs_0_
  31.9 0.0 collective-permute-done.9.refs_2_
  31.9 0.0 collective-permute-done.5.refs_1_
  31.9 0.0 collective-permute-done.11.refs_3_
  31.9 2.1 %score_other.1 = f32[32,4,128]{2,1,0:T(4,128)S(1)} custom-call(bf16[64,1792]{1,0:T(8,128)(2,1)S(1)} %collective-permute-done.3.refs_0_, bf16[64,1792]{1,0:T(8,128)(2,1)S(1)} %collective-permute-done.5.refs_1_, bf16[64,1920]{1,0:T(8,128)(2,1)S(1)} %collective-permute-done.9.refs_2_, bf16[64,1920]{1,0:T(8,128)(2,1)S(1)} %collective-permute-done.11.refs_3_, ...), custom_call_target="tpu_custom_call" | custom-call | flops 1409286144 | bytes 917504 | tf_op jit(solution)/shard_map/score_other/pallas_call | solution.py:252
  34.0 9.2 %all_to_all.5.stats_ref = f32[32,4,128]{2,1,0:T(4,128)S(1)} all-to-all(f32[32,4,128]{2,1,0:T(4,128)S(1)} %score_other.1), channel_id=1, replica_groups=mesh['dp'=16,'vocab'=2] {'dp','vocab'}, dimensions={0} | all-to-all | bytes 131072 | tf_op jit(solution)/shard_map/all_to_all | solution.py:268
  43.2 0.7 %finish.1 = (f32[1,16]{1,0:T(1,128)}, f32[1,1]{1,0:T(1,128)}) custom-call(f32[32,4,128]{2,1,0:T(4,128)S(1)} %all_to_all.5.stats_ref), custom_call_target="tpu_custom_call" | custom-call | tf_op jit(solution)/shard_map/finish/pallas_call | solution.py:269
  (12 shorter events, 0.1 us)
Async XLA Ops:
  1.5 8.3 %collective-permute-start = (bf16[8,1792]{1,0:T(8,128)(2,1)S(1)}, bf16[8,1792]{1,0:T(8,128)(2,1)S(1)}, u32[]{:S(2)}, u32[]{:S(2)}) collective-permute-start(bf16[8,1792]{1,0:T(8,128)(2,1)S(1)} %get-tuple-element.10), channel_id=1, source_target_pairs={{0,16},{2,18},{4,20},{6,22},{8,24},{10,26},{12,28},{14,30},{16,0},... | collective-permute-start | bytes 86024 | tf_op jit(solution)/shard_map/ppermute | solution.py:231
  5.6 5.8 %collective-permute-start.6 = (bf16[8,1920]{1,0:T(8,128)(2,1)S(1)}, bf16[8,1920]{1,0:T(8,128)(2,1)S(1)}, u32[]{:S(2)}, u32[]{:S(2)}) collective-permute-start(bf16[8,1920]{1,0:T(8,128)(2,1)S(1)} %get-tuple-element.11.piece_ref), channel_id=1, source_target_pairs={{0,2},{2,0},{4,6},{6,4},{8,10},{10,8},{12,14},{14,12},{16,18},{18,... | collective-permute-start | bytes 92168 | tf_op jit(solution)/shard_map/ppermute | solution.py:231
  9.8 5.1 %collective-permute-start.1 = (bf16[16,1792]{1,0:T(8,128)(2,1)S(1)}, bf16[16,1792]{1,0:T(8,128)(2,1)S(1)}, u32[]{:S(2)}, u32[]{:S(2)}) collective-permute-start(bf16[16,1792]{1,0:T(8,128)(2,1)S(1)} %pad_maximum_fusion.2), channel_id=1, source_target_pairs={{0,8},{2,10},{4,12},{6,14},{8,0},{10,2},{12,4},{14,6},{16,24},{18,... | collective-permute-start | bytes 172040 | tf_op jit(solution)/shard_map/ppermute | solution.py:231
  11.4 5.7 %collective-permute-start.7 = (bf16[16,1920]{1,0:T(8,128)(2,1)S(1)}, bf16[16,1920]{1,0:T(8,128)(2,1)S(1)}, u32[]{:S(2)}, u32[]{:S(2)}) collective-permute-start(bf16[16,1920]{1,0:T(8,128)(2,1)S(1)} %constant_dynamic-update-slice_fusion.4.piece_ref), channel_id=1, source_target_pairs={{0,16},{2,18},{4,20},{6,22},{8,24},{10,26},{12,28},{14,30},{16,0},... | collective-permute-start | bytes 184328 | tf_op jit(solution)/shard_map/ppermute | solution.py:231
  14.9 8.8 %collective-permute-start.2 = (bf16[32,1792]{1,0:T(8,128)(2,1)S(1)}, bf16[32,1792]{1,0:T(8,128)(2,1)S(1)}, u32[]{:S(2)}, u32[]{:S(2)}) collective-permute-start(bf16[32,1792]{1,0:T(8,128)(2,1)S(1)} %pad_maximum_fusion.1), channel_id=1, source_target_pairs={{0,4},{2,6},{4,0},{6,2},{8,12},{10,14},{12,8},{14,10},{16,20},{18,... | collective-permute-start | bytes 344072 | tf_op jit(solution)/shard_map/ppermute | solution.py:231
  17.2 4.9 %collective-permute-start.8 = (bf16[32,1920]{1,0:T(8,128)(2,1)S(1)}, bf16[32,1920]{1,0:T(8,128)(2,1)S(1)}, u32[]{:S(2)}, u32[]{:S(2)}) collective-permute-start(bf16[32,1920]{1,0:T(8,128)(2,1)S(1)} %pad_maximum_fusion), channel_id=1, source_target_pairs={{0,8},{2,10},{4,12},{6,14},{8,0},{10,2},{12,4},{14,6},{16,24},{18,... | collective-permute-start | bytes 368648 | tf_op jit(solution)/shard_map/ppermute | solution.py:231
  22.1 6.3 %collective-permute-start.10 = (bf16[64,1920]{1,0:T(8,128)(2,1)S(1)}, bf16[64,1920]{1,0:T(8,128)(2,1)S(1)}, u32[]{:S(2)}, u32[]{:S(2)}) collective-permute-start(bf16[64,1920]{1,0:T(8,128)(2,1)S(1)} %constant_dynamic-update-slice_fusion.6.refs_2_), channel_id=1, source_target_pairs={{0,4},{2,6},{4,0},{6,2},{8,12},{10,14},{12,8},{14,10},{16,20},{18,... | collective-permute-start | bytes 737288 | tf_op jit(solution)/shard_map/ppermute | solution.py:231
  23.8 6.1 %collective-permute-start.4 = (bf16[64,1792]{1,0:T(8,128)(2,1)S(1)}, bf16[64,1792]{1,0:T(8,128)(2,1)S(1)}, u32[]{:S(2)}, u32[]{:S(2)}) collective-permute-start(bf16[64,1792]{1,0:T(8,128)(2,1)S(1)} %constant_dynamic-update-slice_fusion.refs_0_), channel_id=1, source_target_pairs={{0,2},{2,0},{4,6},{6,4},{8,10},{10,8},{12,14},{14,12},{16,18},{18,... | collective-permute-start | bytes 688136 | tf_op jit(solution)/shard_map/ppermute | solution.py:231
  24.5 7.4 %collective-permute-start.9 = (bf16[64,1920]{1,0:T(8,128)(2,1)S(1)}, bf16[64,1920]{1,0:T(8,128)(2,1)S(1)}, u32[]{:S(2)}, u32[]{:S(2)}) collective-permute-start(bf16[64,1920]{1,0:T(8,128)(2,1)S(1)} %constant_dynamic-update-slice_fusion.6.refs_2_), channel_id=1, source_target_pairs={{0,1},{1,0},{2,3},{3,2},{4,5},{5,4},{6,7},{7,6},{8,9},{9,8},{10,11... | collective-permute-start | bytes 737288 | tf_op jit(solution)/shard_map/ppermute | solution.py:239
  28.4 3.5 %collective-permute-start.11 = (bf16[64,1920]{1,0:T(8,128)(2,1)S(1)}, bf16[64,1920]{1,0:T(8,128)(2,1)S(1)}, u32[]{:S(2)}, u32[]{:S(2)}) collective-permute-start(bf16[64,1920]{1,0:T(8,128)(2,1)S(1)} %collective-permute-done.10.refs_3_), channel_id=1, source_target_pairs={{0,1},{1,0},{2,3},{3,2},{4,5},{5,4},{6,7},{7,6},{8,9},{9,8},{10,11... | collective-permute-start | bytes 737288 | tf_op jit(solution)/shard_map/ppermute | solution.py:239
  28.4 3.5 %collective-permute-start.3 = (bf16[64,1792]{1,0:T(8,128)(2,1)S(1)}, bf16[64,1792]{1,0:T(8,128)(2,1)S(1)}, u32[]{:S(2)}, u32[]{:S(2)}) collective-permute-start(bf16[64,1792]{1,0:T(8,128)(2,1)S(1)} %constant_dynamic-update-slice_fusion.refs_0_), channel_id=1, source_target_pairs={{0,1},{1,0},{2,3},{3,2},{4,5},{5,4},{6,7},{7,6},{8,9},{9,8},{10,11... | collective-permute-start | bytes 688136 | tf_op jit(solution)/shard_map/ppermute | solution.py:239
  29.8 2.1 %collective-permute-start.5 = (bf16[64,1792]{1,0:T(8,128)(2,1)S(1)}, bf16[64,1792]{1,0:T(8,128)(2,1)S(1)}, u32[]{:S(2)}, u32[]{:S(2)}) collective-permute-start(bf16[64,1792]{1,0:T(8,128)(2,1)S(1)} %collective-permute-done.4.refs_1_), channel_id=1, source_target_pairs={{0,1},{1,0},{2,3},{3,2},{4,5},{5,4},{6,7},{7,6},{8,9},{9,8},{10,11... | collective-permute-start | bytes 688136 | tf_op jit(solution)/shard_map/ppermute | solution.py:239

commit v4 on v3

--- a/solution.py
+++ b/solution.py
@@ -11,7 +11,9 @@
 SUB = 8
 BASE = 256
 DIGITS = 3
-LOADS = (2, 1)
+ORDER = (1, 2, 3)
+SHARE = 0.6
+STEPS = (0, 1)
 TILE = 256
 VMEM = pl.BlockSpec(memory_space=pltpu.VMEM)
 LIMIT = pltpu.CompilerParams(vmem_limit_bytes=20 * 2**20)
@@ -29,7 +31,7 @@
 
 def orders(groups):
     bits = [1 << b for b in reversed(range(groups.bit_length() - 1))]
-    return (bits, bits[-1:] + bits[:-1])
+    return (bits, bits[:-2] + bits[-1:] + bits[-2:-1])
 
 
 def place(order, j):
@@ -222,18 +224,32 @@
 
     steps = len(plan[0])
     weight = None
-    mine = [[piece] for piece in pieces]
-    done = 0
-    for step in range(steps):
+    unit = SUB * CHUNKS
+    first = int(features * SHARE) // unit * unit
+    spans = {STEPS[0]: (0, first), steps - STEPS[1]: (first, features - first)}
+    spans = {s: v for s, v in spans.items() if v[1]}
+    joined = steps - 2
+    whole = jnp.concatenate(pieces, axis=1)
+    for step in range(0, joined, 2):
+        bits = plan[0][step : step + 2]
+        parts = {}
+        for n in ORDER:
+            if n < 1 << len(bits):
+                k = place(bits, n)
+                flips = [(i, i ^ k) for i in range(groups)]
+                parts[n] = lax.ppermute(whole, "dp", flips)
+        if step in spans:
+            weight, whole = load(spans[step], out_weight, whole, weight)
+        parts[0] = whole
+        whole = jnp.concatenate([parts[n] for n in range(len(parts))], axis=0)
+    mine = [[whole[:, :cut]], [whole[:, cut:]]]
+    for step in range(joined, steps):
         for c, order in enumerate(plan):
             flips = [(i, i ^ order[step]) for i in range(groups)]
             whole = jnp.concatenate(mine[c], axis=0)
             mine[c] = [whole, lax.ppermute(whole, "dp", flips)]
-        if step < len(LOADS):
-            size = int((features - done) / LOADS[step])
-            size = size // (SUB * CHUNKS) * SUB * CHUNKS
-            weight, mine[-1][0] = load((done, size), out_weight, whole, weight)
-            done += size
+        if step in spans:
+            weight, mine[-1][0] = load(spans[step], out_weight, whole, weight)
     mine = [part for pair in mine for part in pair]
     swap = [(i, (i + 1) % cores) for i in range(cores)]
     other = [lax.ppermute(part, "vocab", swap) for part in mine]

time: 44.1 us -> 41.8 us (0.948)
  waiting for transfers between devices: 10.4 us -> 8.64 us
  starting transfers between devices: 12.6 us -> 11.5 us
  blocking collectives: 9.16 us -> 9.75 us
    ppermute x8 -> x4, starting transfers between devices: 12.1 us -> 5.19 us  [shards(): mine[c] = [whole, lax.ppermute(whole, 'dp', flips)]]
    ppermute x0 -> x3, starting transfers between devices: none -> 5.71 us  [shards(): parts[n] = lax.ppermute(whole, 'dp', flips)]
    ppermute x8 -> x4, waiting for transfers between devices: 10.4 us -> 5.6 us  [shards(): mine[c] = [whole, lax.ppermute(whole, 'dp', flips)]]
    ppermute x0 -> x3, waiting for transfers between devices: none -> 3.01 us  [shards(): parts[n] = lax.ppermute(whole, 'dp', flips)]
    all_to_all x1, blocking collectives: 9.16 us -> 9.75 us  [shards(): stats = lax.all_to_all(stats, ('dp', 'vocab'), 0, 0)]
  transfers between devices with their start and end apart: 12 -> 11, of which waited for: 4 -> 5; matrix products, arithmetic and copies ran while one was open for 0% -> 0% of each run, Pallas kernels for 17% -> 17%
where the time goes in v4:
time: 41.8 us; the launch traced here: 41.6 us
  starting transfers between devices  11.5 us (28%)
  Pallas kernels  10.8 us (26%)
  blocking collectives  9.75 us (23%)
  waiting for transfers between devices  8.64 us (21%)
  between operations  0.75 us (2%)
    all_to_all x1, blocking collectives, shards(): stats = lax.all_to_all(stats, ('dp', 'vocab'), 0, 0)  9.75 us
    ppermute x3, starting transfers between devices, shards(): parts[n] = lax.ppermute(whole, 'dp', flips)  5.71 us
    ppermute x4, waiting for transfers between devices, shards(): mine[c] = [whole, lax.ppermute(whole, 'dp', flips)]  5.6 us
    pallas_call x2, Pallas kernels, load(): pl.pallas_call(functools.partial(load_kernel, part), out_shape=[jax.Shape...  5.23 us
    ppermute x4, starting transfers between devices, shards(): mine[c] = [whole, lax.ppermute(whole, 'dp', flips)]  5.19 us
    pallas_call x2, Pallas kernels, score(): pl.pallas_call(functools.partial(score_kernel, plan, flip), out_shape=jax...  4.06 us
    ppermute x3, waiting for transfers between devices, shards(): parts[n] = lax.ppermute(whole, 'dp', flips)  3.01 us
    pallas_call x1, Pallas kernels, shards(): pl.pallas_call(functools.partial(pack_kernel, share), out_shape=[jax.Shap...  0.86 us
  transfers between devices with their start and end apart: 11, of which 5 were waited for; matrix products, arithmetic and copies ran while one was open for 0% of the time, Pallas kernels for 17%

profile of v4, /device:TPU:0, one launch (start us, length us, event | category | flops | bytes accessed | tf_op | source)
XLA Modules:
  0.0 41.6 jit_solution(15218271494522787248)
XLA Ops:
  0.6 0.9 %pack.1 = (bf16[8,1792]{1,0:T(8,128)(2,1)S(1)}, bf16[8,1920]{1,0:T(8,128)(2,1)S(1)}) custom-call(s32[16]{0:T(128)} %targets_hbm.1, bf16[16,3584]{1,0:T(8,128)(2,1)} %states_hbm.1), custom_call_target="tpu_custom_call" | custom-call | tf_op jit(solution)/shard_map/pack/pallas_call | solution.py:211
  1.5 4.1 %collective-permute-start = (bf16[8,3712]{1,0:T(8,128)(2,1)S(1)}, bf16[8,3712]{1,0:T(8,128)(2,1)S(1)}, u32[]{:S(2)}, u32[]{:S(2)}) collective-permute-start(bf16[8,3712]{1,0:T(8,128)(2,1)S(1)} %constant_dynamic-update-slice_fusion.piece_ref), channel_id=1, source_target_pairs={{0,16},{2,18},{4,20},{6,22},{8,24},{10,26},{12,28},{14,30},{16,0},... | collective-permute-start | bytes 178184 | tf_op jit(solution)/shard_map/ppermute | solution.py:240
  5.7 1.6 %collective-permute-start.1 = (bf16[8,3712]{1,0:T(8,128)(2,1)S(1)}, bf16[8,3712]{1,0:T(8,128)(2,1)S(1)}, u32[]{:S(2)}, u32[]{:S(2)}) collective-permute-start(bf16[8,3712]{1,0:T(8,128)(2,1)S(1)} %constant_dynamic-update-slice_fusion.piece_ref), channel_id=1, source_target_pairs={{0,8},{2,10},{4,12},{6,14},{8,0},{10,2},{12,4},{14,6},{16,24},{18,... | collective-permute-start | bytes 178184 | tf_op jit(solution)/shard_map/ppermute | solution.py:240
  7.2 0.0 collective-permute-start.2
  7.2 2.9 %load_0.1 = (bf16[3584,1536]{1,0:T(8,128)(2,1)S(1)}, bf16[8,3712]{1,0:T(8,128)(2,1)S(1)}) custom-call(bf16[3584,1536]{1,0:T(8,128)(2,1)} %source.3, bf16[8,3712]{1,0:T(8,128)(2,1)S(1)} %constant_dynamic-update-slice_fusion.piece_ref), custom_call_target="tpu_custom_call" | custom-call | flops 1660944384 | tf_op jit(solution)/shard_map/load_0/pallas_call | solution.py:96
  10.2 0.0 collective-permute-done
  10.2 0.0 collective-permute-done.1
  10.2 3.0 %collective-permute-done.2 = bf16[8,3712]{1,0:T(8,128)(2,1)S(1)} collective-permute-done((bf16[8,3712]{1,0:T(8,128)(2,1)S(1)}, bf16[8,3712]{1,0:T(8,128)(2,1)S(1)}, u32[]{:S(2)}, u32[]{:S(2)}) %collective-permute-start.2) | collective-permute-done | bytes 59424 | tf_op jit(solution)/shard_map/ppermute | solution.py:240
  13.3 1.6 %collective-permute-start.7 = (bf16[32,1920]{1,0:T(8,128)(2,1)S(1)}, bf16[32,1920]{1,0:T(8,128)(2,1)S(1)}, u32[]{:S(2)}, u32[]{:S(2)}) collective-permute-start(bf16[32,1920]{1,0:T(8,128)(2,1)S(1)} %slice.9), channel_id=1, source_target_pairs={{0,2},{2,0},{4,6},{6,4},{8,10},{10,8},{12,14},{14,12},{16,18},{18,... | collective-permute-start | bytes 368648 | tf_op jit(solution)/shard_map/ppermute | solution.py:250
  14.8 1.6 %collective-permute-start.3 = (bf16[32,1792]{1,0:T(8,128)(2,1)S(1)}, bf16[32,1792]{1,0:T(8,128)(2,1)S(1)}, u32[]{:S(2)}, u32[]{:S(2)}) collective-permute-start(bf16[32,1792]{1,0:T(8,128)(2,1)S(1)} %slice.8), channel_id=1, source_target_pairs={{0,4},{2,6},{4,0},{6,2},{8,12},{10,14},{12,8},{14,10},{16,20},{18,... | collective-permute-start | bytes 344072 | tf_op jit(solution)/shard_map/ppermute | solution.py:250
  16.4 1.8 %collective-permute-done.7 = bf16[32,1920]{1,0:T(8,128)(2,1)S(1)} collective-permute-done((bf16[32,1920]{1,0:T(8,128)(2,1)S(1)}, bf16[32,1920]{1,0:T(8,128)(2,1)S(1)}, u32[]{:S(2)}, u32[]{:S(2)}) %collective-permute-start.7) | collective-permute-done | bytes 122912 | tf_op jit(solution)/shard_map/ppermute | solution.py:250
  18.2 1.6 %collective-permute-start.9 = (bf16[64,1920]{1,0:T(8,128)(2,1)S(1)}, bf16[64,1920]{1,0:T(8,128)(2,1)S(1)}, u32[]{:S(2)}, u32[]{:S(2)}) collective-permute-start(bf16[64,1920]{1,0:T(8,128)(2,1)S(1)} %pad_maximum_fusion.piece_ref), channel_id=1, source_target_pairs={{0,4},{2,6},{4,0},{6,2},{8,12},{10,14},{12,8},{14,10},{16,20},{18,... | collective-permute-start | bytes 737288 | tf_op jit(solution)/shard_map/ppermute | solution.py:250
  19.8 1.1 %collective-permute-done.3 = bf16[32,1792]{1,0:T(8,128)(2,1)S(1)} collective-permute-done((bf16[32,1792]{1,0:T(8,128)(2,1)S(1)}, bf16[32,1792]{1,0:T(8,128)(2,1)S(1)}, u32[]{:S(2)}, u32[]{:S(2)}) %collective-permute-start.3) | collective-permute-done | bytes 114720 | tf_op jit(solution)/shard_map/ppermute | solution.py:250
  20.9 0.5 %collective-permute-start.5 = (bf16[64,1792]{1,0:T(8,128)(2,1)S(1)}, bf16[64,1792]{1,0:T(8,128)(2,1)S(1)}, u32[]{:S(2)}, u32[]{:S(2)}) collective-permute-start(bf16[64,1792]{1,0:T(8,128)(2,1)S(1)} %pad_maximum_fusion.1.refs_0_), channel_id=1, source_target_pairs={{0,2},{2,0},{4,6},{6,4},{8,10},{10,8},{12,14},{14,12},{16,18},{18,... | collective-permute-start | bytes 688136 | tf_op jit(solution)/shard_map/ppermute | solution.py:250
  21.4 2.3 %load_2112.1 = (bf16[3584,1536]{1,0:T(8,128)(2,1)S(1)}, bf16[64,1920]{1,0:T(8,128)(2,1)S(1)}) custom-call(bf16[3584,1536]{1,0:T(8,128)(2,1)} %source.3, bf16[64,1920]{1,0:T(8,128)(2,1)S(1)} %pad_maximum_fusion.piece_ref, bf16[3584,1536]{1,0:T(8,128)(2,1)S(1)} %get-tuple-element.13.refs_0_), custom_call_target="tpu_custom_call", output_to_operand_aliasing={{0}: (2, {})} | custom-call | flops 1157627904 | tf_op jit(solution)/shard_map/load_2112/pallas_call | solution.py:96
  23.7 0.1 collective-permute-start.8
  23.8 0.7 %collective-permute-done.9.refs_3_ = bf16[64,1920]{1,0:T(8,128)(2,1)S(1)} collective-permute-done((bf16[64,1920]{1,0:T(8,128)(2,1)S(1)}, bf16[64,1920]{1,0:T(8,128)(2,1)S(1)}, u32[]{:S(2)}, u32[]{:S(2)}) %collective-permute-start.9) | collective-permute-done | bytes 245792 | tf_op jit(solution)/shard_map/ppermute | solution.py:250
  24.5 0.0 collective-permute-start.10
  24.5 0.5 %collective-permute-start.4 = (bf16[64,1792]{1,0:T(8,128)(2,1)S(1)}, bf16[64,1792]{1,0:T(8,128)(2,1)S(1)}, u32[]{:S(2)}, u32[]{:S(2)}) collective-permute-start(bf16[64,1792]{1,0:T(8,128)(2,1)S(1)} %pad_maximum_fusion.1.refs_0_), channel_id=1, source_target_pairs={{0,1},{1,0},{2,3},{3,2},{4,5},{5,4},{6,7},{7,6},{8,9},{9,8},{10,11... | collective-permute-start | bytes 688136 | tf_op jit(solution)/shard_map/ppermute | solution.py:255
  25.0 2.0 %collective-permute-done.5.refs_1_ = bf16[64,1792]{1,0:T(8,128)(2,1)S(1)} collective-permute-done((bf16[64,1792]{1,0:T(8,128)(2,1)S(1)}, bf16[64,1792]{1,0:T(8,128)(2,1)S(1)}, u32[]{:S(2)}, u32[]{:S(2)}) %collective-permute-start.5) | collective-permute-done | bytes 229408 | tf_op jit(solution)/shard_map/ppermute | solution.py:250
  27.0 0.0 collective-permute-start.6
  27.0 2.0 %score_mine.1.refs_5_ = f32[2,128]{1,0:T(2,128)S(1)} custom-call(bf16[64,1792]{1,0:T(8,128)(2,1)S(1)} %pad_maximum_fusion.1.refs_0_, bf16[64,1792]{1,0:T(8,128)(2,1)S(1)} %collective-permute-done.5.refs_1_, bf16[64,1920]{1,0:T(8,128)(2,1)S(1)} %get-tuple-element.14.refs_2_, bf16[64,1920]{1,0:T(8,128)(2,1)S(1)} %collective-permute-done.9.refs_3_, ...), custom_call_target="tpu_custom_call" | custom-call | flops 1409286144 | bytes 917504 | tf_op jit(solution)/shard_map/score_mine/pallas_call | solution.py:268
  29.0 0.0 collective-permute-done.4.refs_0_
  29.0 0.0 collective-permute-done.8.refs_2_
  29.0 0.0 collective-permute-done.6.refs_1_
  29.1 0.0 collective-permute-done.10.refs_3_
  29.1 2.1 %score_other.1 = f32[32,4,128]{2,1,0:T(4,128)S(1)} custom-call(bf16[64,1792]{1,0:T(8,128)(2,1)S(1)} %collective-permute-done.4.refs_0_, bf16[64,1792]{1,0:T(8,128)(2,1)S(1)} %collective-permute-done.6.refs_1_, bf16[64,1920]{1,0:T(8,128)(2,1)S(1)} %collective-permute-done.8.refs_2_, bf16[64,1920]{1,0:T(8,128)(2,1)S(1)} %collective-permute-done.10.refs_3_, ...), custom_call_target="tpu_custom_call" | custom-call | flops 1409286144 | bytes 917504 | tf_op jit(solution)/shard_map/score_other/pallas_call | solution.py:268
  31.1 9.8 %all_to_all.5.stats_ref = f32[32,4,128]{2,1,0:T(4,128)S(1)} all-to-all(f32[32,4,128]{2,1,0:T(4,128)S(1)} %score_other.1), channel_id=1, replica_groups=mesh['dp'=16,'vocab'=2] {'dp','vocab'}, dimensions={0} | all-to-all | bytes 131072 | tf_op jit(solution)/shard_map/all_to_all | solution.py:284
  40.9 0.7 %finish.1 = (f32[1,16]{1,0:T(1,128)}, f32[1,1]{1,0:T(1,128)}) custom-call(f32[32,4,128]{2,1,0:T(4,128)S(1)} %all_to_all.5.stats_ref), custom_call_target="tpu_custom_call" | custom-call | tf_op jit(solution)/shard_map/finish/pallas_call | solution.py:285
  (10 shorter events, 0.1 us)
Async XLA Ops:
  1.5 8.7 %collective-permute-start = (bf16[8,3712]{1,0:T(8,128)(2,1)S(1)}, bf16[8,3712]{1,0:T(8,128)(2,1)S(1)}, u32[]{:S(2)}, u32[]{:S(2)}) collective-permute-start(bf16[8,3712]{1,0:T(8,128)(2,1)S(1)} %constant_dynamic-update-slice_fusion.piece_ref), channel_id=1, source_target_pairs={{0,16},{2,18},{4,20},{6,22},{8,24},{10,26},{12,28},{14,30},{16,0},... | collective-permute-start | bytes 178184 | tf_op jit(solution)/shard_map/ppermute | solution.py:240
  5.7 4.5 %collective-permute-start.1 = (bf16[8,3712]{1,0:T(8,128)(2,1)S(1)}, bf16[8,3712]{1,0:T(8,128)(2,1)S(1)}, u32[]{:S(2)}, u32[]{:S(2)}) collective-permute-start(bf16[8,3712]{1,0:T(8,128)(2,1)S(1)} %constant_dynamic-update-slice_fusion.piece_ref), channel_id=1, source_target_pairs={{0,8},{2,10},{4,12},{6,14},{8,0},{10,2},{12,4},{14,6},{16,24},{18,... | collective-permute-start | bytes 178184 | tf_op jit(solution)/shard_map/ppermute | solution.py:240
  7.2 6.0 %collective-permute-start.2 = (bf16[8,3712]{1,0:T(8,128)(2,1)S(1)}, bf16[8,3712]{1,0:T(8,128)(2,1)S(1)}, u32[]{:S(2)}, u32[]{:S(2)}) collective-permute-start(bf16[8,3712]{1,0:T(8,128)(2,1)S(1)} %constant_dynamic-update-slice_fusion.piece_ref), channel_id=1, source_target_pairs={{0,24},{2,26},{4,28},{6,30},{8,16},{10,18},{12,20},{14,22},{16,8},... | collective-permute-start | bytes 178184 | tf_op jit(solution)/shard_map/ppermute | solution.py:240
  13.3 4.9 %collective-permute-start.7 = (bf16[32,1920]{1,0:T(8,128)(2,1)S(1)}, bf16[32,1920]{1,0:T(8,128)(2,1)S(1)}, u32[]{:S(2)}, u32[]{:S(2)}) collective-permute-start(bf16[32,1920]{1,0:T(8,128)(2,1)S(1)} %slice.9), channel_id=1, source_target_pairs={{0,2},{2,0},{4,6},{6,4},{8,10},{10,8},{12,14},{14,12},{16,18},{18,... | collective-permute-start | bytes 368648 | tf_op jit(solution)/shard_map/ppermute | solution.py:250
  14.8 6.1 %collective-permute-start.3 = (bf16[32,1792]{1,0:T(8,128)(2,1)S(1)}, bf16[32,1792]{1,0:T(8,128)(2,1)S(1)}, u32[]{:S(2)}, u32[]{:S(2)}) collective-permute-start(bf16[32,1792]{1,0:T(8,128)(2,1)S(1)} %slice.8), channel_id=1, source_target_pairs={{0,4},{2,6},{4,0},{6,2},{8,12},{10,14},{12,8},{14,10},{16,20},{18,... | collective-permute-start | bytes 344072 | tf_op jit(solution)/shard_map/ppermute | solution.py:250
  18.2 6.3 %collective-permute-start.9 = (bf16[64,1920]{1,0:T(8,128)(2,1)S(1)}, bf16[64,1920]{1,0:T(8,128)(2,1)S(1)}, u32[]{:S(2)}, u32[]{:S(2)}) collective-permute-start(bf16[64,1920]{1,0:T(8,128)(2,1)S(1)} %pad_maximum_fusion.piece_ref), channel_id=1, source_target_pairs={{0,4},{2,6},{4,0},{6,2},{8,12},{10,14},{12,8},{14,10},{16,20},{18,... | collective-permute-start | bytes 737288 | tf_op jit(solution)/shard_map/ppermute | solution.py:250
  20.9 6.1 %collective-permute-start.5 = (bf16[64,1792]{1,0:T(8,128)(2,1)S(1)}, bf16[64,1792]{1,0:T(8,128)(2,1)S(1)}, u32[]{:S(2)}, u32[]{:S(2)}) collective-permute-start(bf16[64,1792]{1,0:T(8,128)(2,1)S(1)} %pad_maximum_fusion.1.refs_0_), channel_id=1, source_target_pairs={{0,2},{2,0},{4,6},{6,4},{8,10},{10,8},{12,14},{14,12},{16,18},{18,... | collective-permute-start | bytes 688136 | tf_op jit(solution)/shard_map/ppermute | solution.py:250
  23.7 5.3 %collective-permute-start.8 = (bf16[64,1920]{1,0:T(8,128)(2,1)S(1)}, bf16[64,1920]{1,0:T(8,128)(2,1)S(1)}, u32[]{:S(2)}, u32[]{:S(2)}) collective-permute-start(bf16[64,1920]{1,0:T(8,128)(2,1)S(1)} %get-tuple-element.14.refs_2_), channel_id=1, source_target_pairs={{0,1},{1,0},{2,3},{3,2},{4,5},{5,4},{6,7},{7,6},{8,9},{9,8},{10,11... | collective-permute-start | bytes 737288 | tf_op jit(solution)/shard_map/ppermute | solution.py:255
  24.5 4.6 %collective-permute-start.10 = (bf16[64,1920]{1,0:T(8,128)(2,1)S(1)}, bf16[64,1920]{1,0:T(8,128)(2,1)S(1)}, u32[]{:S(2)}, u32[]{:S(2)}) collective-permute-start(bf16[64,1920]{1,0:T(8,128)(2,1)S(1)} %collective-permute-done.9.refs_3_), channel_id=1, source_target_pairs={{0,1},{1,0},{2,3},{3,2},{4,5},{5,4},{6,7},{7,6},{8,9},{9,8},{10,11... | collective-permute-start | bytes 737288 | tf_op jit(solution)/shard_map/ppermute | solution.py:255
  24.5 4.5 %collective-permute-start.4 = (bf16[64,1792]{1,0:T(8,128)(2,1)S(1)}, bf16[64,1792]{1,0:T(8,128)(2,1)S(1)}, u32[]{:S(2)}, u32[]{:S(2)}) collective-permute-start(bf16[64,1792]{1,0:T(8,128)(2,1)S(1)} %pad_maximum_fusion.1.refs_0_), channel_id=1, source_target_pairs={{0,1},{1,0},{2,3},{3,2},{4,5},{5,4},{6,7},{7,6},{8,9},{9,8},{10,11... | collective-permute-start | bytes 688136 | tf_op jit(solution)/shard_map/ppermute | solution.py:255
  27.0 2.0 %collective-permute-start.6 = (bf16[64,1792]{1,0:T(8,128)(2,1)S(1)}, bf16[64,1792]{1,0:T(8,128)(2,1)S(1)}, u32[]{:S(2)}, u32[]{:S(2)}) collective-permute-start(bf16[64,1792]{1,0:T(8,128)(2,1)S(1)} %collective-permute-done.5.refs_1_), channel_id=1, source_target_pairs={{0,1},{1,0},{2,3},{3,2},{4,5},{5,4},{6,7},{7,6},{8,9},{9,8},{10,11... | collective-permute-start | bytes 688136 | tf_op jit(solution)/shard_map/ppermute | solution.py:255

commit v5 on v3

--- a/solution.py
+++ b/solution.py
@@ -11,7 +11,10 @@
 SUB = 8
 BASE = 256
 DIGITS = 3
-LOADS = (2, 1)
+PARTS = 4
+ORDER = (1, 2, 3)
+SHARE = 0.5
+STEPS = (0, 1)
 TILE = 256
 VMEM = pl.BlockSpec(memory_space=pltpu.VMEM)
 LIMIT = pltpu.CompilerParams(vmem_limit_bytes=20 * 2**20)
@@ -29,7 +32,7 @@
 
 def orders(groups):
     bits = [1 << b for b in reversed(range(groups.bit_length() - 1))]
-    return (bits, bits[-1:] + bits[:-1])
+    return bits
 
 
 def place(order, j):
@@ -112,7 +115,7 @@
 
 
 def score_kernel(plan, flip, *refs):
-    pieces, rest = refs[: 2 * len(plan)], list(refs[2 * len(plan) :])
+    pieces, rest = refs[:PARTS], list(refs[PARTS:])
     weight_ref = rest.pop(0)
     before_ref = rest.pop(0) if flip else None
     out_ref, rows_ref, logits_ref, stats_ref = rest
@@ -120,16 +123,9 @@
     rows = rows_ref.shape[0]
     group, core = lax.axis_index("dp"), lax.axis_index("vocab")
     cores = lax.axis_size("vocab")
-    at = 0
-    for c, order in enumerate(plan):
-        early, late = pieces[2 * c : 2 * c + 2]
-        width = early.shape[1]
-        for j in range(rows // SUB):
-            to = place(order, j) * SUB
-            ref = early if j < rows // SUB // 2 else late
-            at_row = j * SUB % (rows // 2)
-            rows_ref[to : to + SUB, at : at + width] = ref[at_row : at_row + SUB, :]
-        at += width
+    size = rows // len(pieces)
+    for n, ref in enumerate(pieces):
+        rows_ref[n * size : (n + 1) * size, :] = ref[...]
     states = rows_ref[:, :features]
 
     def multiply(n, top):
@@ -163,7 +159,7 @@
     picked = jnp.sum(picked, axis=1, keepdims=True)
     stats = jnp.where(lane == 0, norm, jnp.where(lane == 1, picked, 0.0))
     for j in range(rows // SUB):
-        to = pl.multiple_of((group ^ j) * SUB, SUB)
+        to = pl.multiple_of((group ^ place(plan, j)) * SUB, SUB)
         stats_ref[pl.ds(to, SUB), :] = stats[j * SUB : (j + 1) * SUB, :]
     stats = stats_ref[...].T[:2, :]
     if not flip:
@@ -202,15 +198,13 @@
     half = groups * share
     dtype = hidden_states.dtype
     plan = orders(groups)
-    cut = features // len(plan) // LANES * LANES
-    widths = [cut] * (len(plan) - 1)
-    widths.append(features - sum(widths) + LANES)
+    width = features + LANES
 
     pieces = pl.pallas_call(
         functools.partial(pack_kernel, share),
-        out_shape=[jax.ShapeDtypeStruct((share, w), dtype) for w in widths],
+        out_shape=[jax.ShapeDtypeStruct((share, width), dtype)],
         in_specs=[HBM, HBM],
-        out_specs=[VMEM] * len(widths),
+        out_specs=[VMEM],
         scratch_shapes=[
             pltpu.SMEM((local_tokens,), jnp.int32),
             pltpu.VMEM((share, features), dtype),
@@ -220,21 +214,23 @@
         name="pack",
     )(far(targets), far(hidden_states))
 
-    steps = len(plan[0])
+    steps = len(plan)
     weight = None
-    mine = [[piece] for piece in pieces]
-    done = 0
-    for step in range(steps):
-        for c, order in enumerate(plan):
-            flips = [(i, i ^ order[step]) for i in range(groups)]
-            whole = jnp.concatenate(mine[c], axis=0)
-            mine[c] = [whole, lax.ppermute(whole, "dp", flips)]
-        if step < len(LOADS):
-            size = int((features - done) / LOADS[step])
-            size = size // (SUB * CHUNKS) * SUB * CHUNKS
-            weight, mine[-1][0] = load((done, size), out_weight, whole, weight)
-            done += size
-    mine = [part for pair in mine for part in pair]
+    unit = SUB * CHUNKS
+    first = int(features * SHARE) // unit * unit
+    spans = {0: (0, first), steps - 2: (first, features - first)}
+    (whole,) = pieces
+    for step in range(0, steps, 2):
+        bits = plan[step : step + 2]
+        mine = [whole]
+        for n in range(1, 1 << len(bits)):
+            k = place(bits, n)
+            flips = [(i, i ^ k) for i in range(groups)]
+            mine.append(lax.ppermute(whole, "dp", flips))
+        if step in spans:
+            weight, mine[0] = load(spans[step], out_weight, whole, weight)
+        if step + 2 < steps:
+            whole = jnp.concatenate(mine, axis=0)
     swap = [(i, (i + 1) % cores) for i in range(cores)]
     other = [lax.ppermute(part, "vocab", swap) for part in mine]
 

time: 44.1 us -> 41.1 us (0.932)
  starting transfers between devices: 12.6 us -> 9.92 us
  waiting for transfers between devices: 10.4 us -> 8.46 us
  blocking collectives: 9.16 us -> 10.9 us
    ppermute x8 -> x6, starting transfers between devices: 12.1 us -> 9.34 us  [shards(): mine.append(lax.ppermute(whole, 'dp', flips))]
    ppermute x8 -> x6, waiting for transfers between devices: 10.4 us -> 8.42 us  [shards(): mine.append(lax.ppermute(whole, 'dp', flips))]
    all_to_all x1, blocking collectives: 9.16 us -> 10.9 us  [shards(): stats = lax.all_to_all(stats, ('dp', 'vocab'), 0, 0)]
  transfers between devices with their start and end apart: 12 -> 10, of which waited for: 4 -> 3; matrix products, arithmetic and copies ran while one was open for 0% -> 0% of each run, Pallas kernels for 17% -> 18%
where the time goes in v5:
time: 41.1 us; the launch traced here: 40.9 us
  Pallas kernels  10.9 us (27%)
  blocking collectives  10.9 us (27%)
  starting transfers between devices  9.92 us (24%)
  waiting for transfers between devices  8.46 us (21%)
  between operations  0.72 us (2%)
    all_to_all x1, blocking collectives, shards(): stats = lax.all_to_all(stats, ('dp', 'vocab'), 0, 0)  10.9 us
    ppermute x6, starting transfers between devices, shards(): mine.append(lax.ppermute(whole, 'dp', flips))  9.34 us
    ppermute x6, waiting for transfers between devices, shards(): mine.append(lax.ppermute(whole, 'dp', flips))  8.42 us
    pallas_call x2, Pallas kernels, load(): pl.pallas_call(functools.partial(load_kernel, part), out_shape=[jax.Shape...  5.24 us
    pallas_call x2, Pallas kernels, score(): pl.pallas_call(functools.partial(score_kernel, plan, flip), out_shape=jax...  4.11 us
    pallas_call x1, Pallas kernels, shards(): pl.pallas_call(functools.partial(pack_kernel, share), out_shape=[jax.Shap...  0.86 us
  transfers between devices with their start and end apart: 10, of which 3 were waited for; matrix products, arithmetic and copies ran while one was open for 0% of the time, Pallas kernels for 18%

profile of v5, /device:TPU:0, one launch (start us, length us, event | category | flops | bytes accessed | tf_op | source)
XLA Modules:
  0.0 40.9 jit_solution(14457085428155657533)
XLA Ops:
  0.6 0.9 %pack.1.piece_ref = bf16[8,3712]{1,0:T(8,128)(2,1)S(1)} custom-call(s32[16]{0:T(128)} %targets_hbm.1, bf16[16,3584]{1,0:T(8,128)(2,1)} %states_hbm.1), custom_call_target="tpu_custom_call" | custom-call | tf_op jit(solution)/shard_map/pack/pallas_call | solution.py:203
  1.5 5.1 %collective-permute-start.2 = (bf16[8,3712]{1,0:T(8,128)(2,1)S(1)}, bf16[8,3712]{1,0:T(8,128)(2,1)S(1)}, u32[]{:S(2)}, u32[]{:S(2)}) collective-permute-start(bf16[8,3712]{1,0:T(8,128)(2,1)S(1)} %pack.1.piece_ref), channel_id=1, source_target_pairs={{0,24},{2,26},{4,28},{6,30},{8,16},{10,18},{12,20},{14,22},{16,8},... | collective-permute-start | bytes 178184 | tf_op jit(solution)/shard_map/ppermute | solution.py:229
  6.6 0.0 collective-permute-start.1
  6.6 0.6 %collective-permute-start = (bf16[8,3712]{1,0:T(8,128)(2,1)S(1)}, bf16[8,3712]{1,0:T(8,128)(2,1)S(1)}, u32[]{:S(2)}, u32[]{:S(2)}) collective-permute-start(bf16[8,3712]{1,0:T(8,128)(2,1)S(1)} %pack.1.piece_ref), channel_id=1, source_target_pairs={{0,16},{2,18},{4,20},{6,22},{8,24},{10,26},{12,28},{14,30},{16,0},... | collective-permute-start | bytes 178184 | tf_op jit(solution)/shard_map/ppermute | solution.py:229
  7.3 2.6 %load_0.1 = (bf16[3584,1536]{1,0:T(8,128)(2,1)S(1)}, bf16[8,3712]{1,0:T(8,128)(2,1)S(1)}) custom-call(bf16[3584,1536]{1,0:T(8,128)(2,1)} %source.3, bf16[8,3712]{1,0:T(8,128)(2,1)S(1)} %pack.1.piece_ref), custom_call_target="tpu_custom_call" | custom-call | flops 1409286144 | tf_op jit(solution)/shard_map/load_0/pallas_call | solution.py:97
  9.9 2.2 %collective-permute-done = bf16[8,3712]{1,0:T(8,128)(2,1)S(1)} collective-permute-done((bf16[8,3712]{1,0:T(8,128)(2,1)S(1)}, bf16[8,3712]{1,0:T(8,128)(2,1)S(1)}, u32[]{:S(2)}, u32[]{:S(2)}) %collective-permute-start) | collective-permute-done | bytes 59424 | tf_op jit(solution)/shard_map/ppermute | solution.py:229
  12.2 0.0 collective-permute-done.1
  12.2 0.0 collective-permute-done.2
  12.2 2.5 %collective-permute-start.8 = (bf16[32,3712]{1,0:T(8,128)(2,1)S(1)}, bf16[32,3712]{1,0:T(8,128)(2,1)S(1)}, u32[]{:S(2)}, u32[]{:S(2)}) collective-permute-start(bf16[32,3712]{1,0:T(8,128)(2,1)S(1)} %constant_dynamic-update-slice_fusion.piece_ref), channel_id=1, source_target_pairs={{0,6},{2,4},{4,2},{6,0},{8,14},{10,12},{12,10},{14,8},{16,22},{18,... | collective-permute-start | bytes 712712 | tf_op jit(solution)/shard_map/ppermute | solution.py:229
  14.7 0.5 %collective-permute-start.6 = (bf16[32,3712]{1,0:T(8,128)(2,1)S(1)}, bf16[32,3712]{1,0:T(8,128)(2,1)S(1)}, u32[]{:S(2)}, u32[]{:S(2)}) collective-permute-start(bf16[32,3712]{1,0:T(8,128)(2,1)S(1)} %constant_dynamic-update-slice_fusion.piece_ref), channel_id=1, source_target_pairs={{0,2},{2,0},{4,6},{6,4},{8,10},{10,8},{12,14},{14,12},{16,18},{18,... | collective-permute-start | bytes 712712 | tf_op jit(solution)/shard_map/ppermute | solution.py:229
  15.2 0.5 %collective-permute-start.4 = (bf16[32,3712]{1,0:T(8,128)(2,1)S(1)}, bf16[32,3712]{1,0:T(8,128)(2,1)S(1)}, u32[]{:S(2)}, u32[]{:S(2)}) collective-permute-start(bf16[32,3712]{1,0:T(8,128)(2,1)S(1)} %constant_dynamic-update-slice_fusion.piece_ref), channel_id=1, source_target_pairs={{0,4},{2,6},{4,0},{6,2},{8,12},{10,14},{12,8},{14,10},{16,20},{18,... | collective-permute-start | bytes 712712 | tf_op jit(solution)/shard_map/ppermute | solution.py:229
  15.8 2.6 %load_1792.1 = (bf16[3584,1536]{1,0:T(8,128)(2,1)S(1)}, bf16[32,3712]{1,0:T(8,128)(2,1)S(1)}) custom-call(bf16[3584,1536]{1,0:T(8,128)(2,1)} %source.3, bf16[32,3712]{1,0:T(8,128)(2,1)S(1)} %constant_dynamic-update-slice_fusion.piece_ref, bf16[3584,1536]{1,0:T(8,128)(2,1)S(1)} %get-tuple-element.9.refs_0_), custom_call_target="tpu_custom_call", output_to_operand_aliasing={{0}: (2, {})} | custom-call | flops 1409286144 | tf_op jit(solution)/shard_map/load_1792/pallas_call | solution.py:97
  18.4 0.1 collective-permute-start.3
  18.5 3.4 %collective-permute-done.8.refs_3_ = bf16[32,3712]{1,0:T(8,128)(2,1)S(1)} collective-permute-done((bf16[32,3712]{1,0:T(8,128)(2,1)S(1)}, bf16[32,3712]{1,0:T(8,128)(2,1)S(1)}, u32[]{:S(2)}, u32[]{:S(2)}) %collective-permute-start.8) | collective-permute-done | bytes 237600 | tf_op jit(solution)/shard_map/ppermute | solution.py:229
  21.8 0.0 collective-permute-start.9
  21.8 2.8 %collective-permute-done.6.refs_2_ = bf16[32,3712]{1,0:T(8,128)(2,1)S(1)} collective-permute-done((bf16[32,3712]{1,0:T(8,128)(2,1)S(1)}, bf16[32,3712]{1,0:T(8,128)(2,1)S(1)}, u32[]{:S(2)}, u32[]{:S(2)}) %collective-permute-start.6) | collective-permute-done | bytes 237600 | tf_op jit(solution)/shard_map/ppermute | solution.py:229
  24.7 0.0 collective-permute-start.7
  24.7 0.0 collective-permute-done.4.refs_1_
  24.7 0.5 %collective-permute-start.5 = (bf16[32,3712]{1,0:T(8,128)(2,1)S(1)}, bf16[32,3712]{1,0:T(8,128)(2,1)S(1)}, u32[]{:S(2)}, u32[]{:S(2)}) collective-permute-start(bf16[32,3712]{1,0:T(8,128)(2,1)S(1)} %collective-permute-done.4.refs_1_), channel_id=1, source_target_pairs={{0,1},{1,0},{2,3},{3,2},{4,5},{5,4},{6,7},{7,6},{8,9},{9,8},{10,11... | collective-permute-start | bytes 712712 | tf_op jit(solution)/shard_map/ppermute | solution.py:235
  25.2 2.0 %score_mine.1.refs_5_ = f32[2,128]{1,0:T(2,128)S(1)} custom-call(bf16[32,3712]{1,0:T(8,128)(2,1)S(1)} %get-tuple-element.10.refs_0_, bf16[32,3712]{1,0:T(8,128)(2,1)S(1)} %collective-permute-done.4.refs_1_, bf16[32,3712]{1,0:T(8,128)(2,1)S(1)} %collective-permute-done.6.refs_2_, bf16[32,3712]{1,0:T(8,128)(2,1)S(1)} %collective-permute-done.8.refs_3_, ...), custom_call_target="tpu_custom_call" | custom-call | flops 1409286144 | bytes 917504 | tf_op jit(solution)/shard_map/score_mine/pallas_call | solution.py:248
  27.2 0.0 collective-permute-done.3.refs_0_
  27.2 0.0 collective-permute-done.9.refs_3_
  27.2 0.0 collective-permute-done.7.refs_2_
  27.2 0.0 collective-permute-done.5.refs_1_
  27.3 2.1 %score_other.1 = f32[32,4,128]{2,1,0:T(4,128)S(1)} custom-call(bf16[32,3712]{1,0:T(8,128)(2,1)S(1)} %collective-permute-done.3.refs_0_, bf16[32,3712]{1,0:T(8,128)(2,1)S(1)} %collective-permute-done.5.refs_1_, bf16[32,3712]{1,0:T(8,128)(2,1)S(1)} %collective-permute-done.7.refs_2_, bf16[32,3712]{1,0:T(8,128)(2,1)S(1)} %collective-permute-done.9.refs_3_, ...), custom_call_target="tpu_custom_call" | custom-call | flops 1409286144 | bytes 917504 | tf_op jit(solution)/shard_map/score_other/pallas_call | solution.py:248
  29.4 10.9 %all_to_all.5.stats_ref = f32[32,4,128]{2,1,0:T(4,128)S(1)} all-to-all(f32[32,4,128]{2,1,0:T(4,128)S(1)} %score_other.1), channel_id=1, replica_groups=mesh['dp'=16,'vocab'=2] {'dp','vocab'}, dimensions={0} | all-to-all | bytes 131072 | tf_op jit(solution)/shard_map/all_to_all | solution.py:264
  40.2 0.7 %finish.1 = (f32[1,16]{1,0:T(1,128)}, f32[1,1]{1,0:T(1,128)}) custom-call(f32[32,4,128]{2,1,0:T(4,128)S(1)} %all_to_all.5.stats_ref), custom_call_target="tpu_custom_call" | custom-call | tf_op jit(solution)/shard_map/finish/pallas_call | solution.py:265
  (4 shorter events, 0.0 us)
Async XLA Ops:
  1.5 10.7 %collective-permute-start.2 = (bf16[8,3712]{1,0:T(8,128)(2,1)S(1)}, bf16[8,3712]{1,0:T(8,128)(2,1)S(1)}, u32[]{:S(2)}, u32[]{:S(2)}) collective-permute-start(bf16[8,3712]{1,0:T(8,128)(2,1)S(1)} %pack.1.piece_ref), channel_id=1, source_target_pairs={{0,24},{2,26},{4,28},{6,30},{8,16},{10,18},{12,20},{14,22},{16,8},... | collective-permute-start | bytes 178184 | tf_op jit(solution)/shard_map/ppermute | solution.py:229
  6.6 5.5 %collective-permute-start.1 = (bf16[8,3712]{1,0:T(8,128)(2,1)S(1)}, bf16[8,3712]{1,0:T(8,128)(2,1)S(1)}, u32[]{:S(2)}, u32[]{:S(2)}) collective-permute-start(bf16[8,3712]{1,0:T(8,128)(2,1)S(1)} %pack.1.piece_ref), channel_id=1, source_target_pairs={{0,8},{2,10},{4,12},{6,14},{8,0},{10,2},{12,4},{14,6},{16,24},{18,... | collective-permute-start | bytes 178184 | tf_op jit(solution)/shard_map/ppermute | solution.py:229
  6.6 5.5 %collective-permute-start = (bf16[8,3712]{1,0:T(8,128)(2,1)S(1)}, bf16[8,3712]{1,0:T(8,128)(2,1)S(1)}, u32[]{:S(2)}, u32[]{:S(2)}) collective-permute-start(bf16[8,3712]{1,0:T(8,128)(2,1)S(1)} %pack.1.piece_ref), channel_id=1, source_target_pairs={{0,16},{2,18},{4,20},{6,22},{8,24},{10,26},{12,28},{14,30},{16,0},... | collective-permute-start | bytes 178184 | tf_op jit(solution)/shard_map/ppermute | solution.py:229
  12.2 9.6 %collective-permute-start.8 = (bf16[32,3712]{1,0:T(8,128)(2,1)S(1)}, bf16[32,3712]{1,0:T(8,128)(2,1)S(1)}, u32[]{:S(2)}, u32[]{:S(2)}) collective-permute-start(bf16[32,3712]{1,0:T(8,128)(2,1)S(1)} %constant_dynamic-update-slice_fusion.piece_ref), channel_id=1, source_target_pairs={{0,6},{2,4},{4,2},{6,0},{8,14},{10,12},{12,10},{14,8},{16,22},{18,... | collective-permute-start | bytes 712712 | tf_op jit(solution)/shard_map/ppermute | solution.py:229
  14.7 10.0 %collective-permute-start.6 = (bf16[32,3712]{1,0:T(8,128)(2,1)S(1)}, bf16[32,3712]{1,0:T(8,128)(2,1)S(1)}, u32[]{:S(2)}, u32[]{:S(2)}) collective-permute-start(bf16[32,3712]{1,0:T(8,128)(2,1)S(1)} %constant_dynamic-update-slice_fusion.piece_ref), channel_id=1, source_target_pairs={{0,2},{2,0},{4,6},{6,4},{8,10},{10,8},{12,14},{14,12},{16,18},{18,... | collective-permute-start | bytes 712712 | tf_op jit(solution)/shard_map/ppermute | solution.py:229
  15.2 9.4 %collective-permute-start.4 = (bf16[32,3712]{1,0:T(8,128)(2,1)S(1)}, bf16[32,3712]{1,0:T(8,128)(2,1)S(1)}, u32[]{:S(2)}, u32[]{:S(2)}) collective-permute-start(bf16[32,3712]{1,0:T(8,128)(2,1)S(1)} %constant_dynamic-update-slice_fusion.piece_ref), channel_id=1, source_target_pairs={{0,4},{2,6},{4,0},{6,2},{8,12},{10,14},{12,8},{14,10},{16,20},{18,... | collective-permute-start | bytes 712712 | tf_op jit(solution)/shard_map/ppermute | solution.py:229
  18.4 8.8 %collective-permute-start.3 = (bf16[32,3712]{1,0:T(8,128)(2,1)S(1)}, bf16[32,3712]{1,0:T(8,128)(2,1)S(1)}, u32[]{:S(2)}, u32[]{:S(2)}) collective-permute-start(bf16[32,3712]{1,0:T(8,128)(2,1)S(1)} %get-tuple-element.10.refs_0_), channel_id=1, source_target_pairs={{0,1},{1,0},{2,3},{3,2},{4,5},{5,4},{6,7},{7,6},{8,9},{9,8},{10,11... | collective-permute-start | bytes 712712 | tf_op jit(solution)/shard_map/ppermute | solution.py:235
  21.8 5.4 %collective-permute-start.9 = (bf16[32,3712]{1,0:T(8,128)(2,1)S(1)}, bf16[32,3712]{1,0:T(8,128)(2,1)S(1)}, u32[]{:S(2)}, u32[]{:S(2)}) collective-permute-start(bf16[32,3712]{1,0:T(8,128)(2,1)S(1)} %collective-permute-done.8.refs_3_), channel_id=1, source_target_pairs={{0,1},{1,0},{2,3},{3,2},{4,5},{5,4},{6,7},{7,6},{8,9},{9,8},{10,11... | collective-permute-start | bytes 712712 | tf_op jit(solution)/shard_map/ppermute | solution.py:235
  24.7 2.6 %collective-permute-start.7 = (bf16[32,3712]{1,0:T(8,128)(2,1)S(1)}, bf16[32,3712]{1,0:T(8,128)(2,1)S(1)}, u32[]{:S(2)}, u32[]{:S(2)}) collective-permute-start(bf16[32,3712]{1,0:T(8,128)(2,1)S(1)} %collective-permute-done.6.refs_2_), channel_id=1, source_target_pairs={{0,1},{1,0},{2,3},{3,2},{4,5},{5,4},{6,7},{7,6},{8,9},{9,8},{10,11... | collective-permute-start | bytes 712712 | tf_op jit(solution)/shard_map/ppermute | solution.py:235
  24.7 2.6 %collective-permute-start.5 = (bf16[32,3712]{1,0:T(8,128)(2,1)S(1)}, bf16[32,3712]{1,0:T(8,128)(2,1)S(1)}, u32[]{:S(2)}, u32[]{:S(2)}) collective-permute-start(bf16[32,3712]{1,0:T(8,128)(2,1)S(1)} %collective-permute-done.4.refs_1_), channel_id=1, source_target_pairs={{0,1},{1,0},{2,3},{3,2},{4,5},{5,4},{6,7},{7,6},{8,9},{9,8},{10,11... | collective-permute-start | bytes 712712 | tf_op jit(solution)/shard_map/ppermute | solution.py:235

commit v6 on v5

--- a/solution.py
+++ b/solution.py
@@ -13,7 +13,7 @@
 DIGITS = 3
 PARTS = 4
 ORDER = (1, 2, 3)
-SHARE = 0.5
+SHARE = 0.3
 STEPS = (0, 1)
 TILE = 256
 VMEM = pl.BlockSpec(memory_space=pltpu.VMEM)

time: 41.1 us -> 40.9 us (level)
  no operation moved by 1% of the time
where the time goes in v6:
time: 40.9 us; the launch traced here: 40.7 us
  Pallas kernels  10.9 us (27%)
  blocking collectives  10.7 us (26%)
  starting transfers between devices  9.92 us (24%)
  waiting for transfers between devices  8.48 us (21%)
  between operations  0.72 us (2%)
    all_to_all x1, blocking collectives, shards(): stats = lax.all_to_all(stats, ('dp', 'vocab'), 0, 0)  10.7 us
    ppermute x6, starting transfers between devices, shards(): mine.append(lax.ppermute(whole, 'dp', flips))  9.34 us
    ppermute x6, waiting for transfers between devices, shards(): mine.append(lax.ppermute(whole, 'dp', flips))  8.45 us
    pallas_call x2, Pallas kernels, load(): pl.pallas_call(functools.partial(load_kernel, part), out_shape=[jax.Shape...  5.21 us
    pallas_call x2, Pallas kernels, score(): pl.pallas_call(functools.partial(score_kernel, plan, flip), out_shape=jax...  4.11 us
    pallas_call x1, Pallas kernels, shards(): pl.pallas_call(functools.partial(pack_kernel, share), out_shape=[jax.Shap...  0.86 us
  transfers between devices with their start and end apart: 10, of which 3 were waited for; matrix products, arithmetic and copies ran while one was open for 0% of the time, Pallas kernels for 18%

profile of v6, /device:TPU:0, one launch (start us, length us, event | category | flops | bytes accessed | tf_op | source)
XLA Modules:
  0.0 40.7 jit_solution(17569768060716555295)
XLA Ops:
  0.6 0.9 %pack.1.piece_ref = bf16[8,3712]{1,0:T(8,128)(2,1)S(1)} custom-call(s32[16]{0:T(128)} %targets_hbm.1, bf16[16,3584]{1,0:T(8,128)(2,1)} %states_hbm.1), custom_call_target="tpu_custom_call" | custom-call | tf_op jit(solution)/shard_map/pack/pallas_call | solution.py:203
  1.5 5.1 %collective-permute-start.2 = (bf16[8,3712]{1,0:T(8,128)(2,1)S(1)}, bf16[8,3712]{1,0:T(8,128)(2,1)S(1)}, u32[]{:S(2)}, u32[]{:S(2)}) collective-permute-start(bf16[8,3712]{1,0:T(8,128)(2,1)S(1)} %pack.1.piece_ref), channel_id=1, source_target_pairs={{0,24},{2,26},{4,28},{6,30},{8,16},{10,18},{12,20},{14,22},{16,8},... | collective-permute-start | bytes 178184 | tf_op jit(solution)/shard_map/ppermute | solution.py:229
  6.6 0.0 collective-permute-start.1
  6.6 0.6 %collective-permute-start = (bf16[8,3712]{1,0:T(8,128)(2,1)S(1)}, bf16[8,3712]{1,0:T(8,128)(2,1)S(1)}, u32[]{:S(2)}, u32[]{:S(2)}) collective-permute-start(bf16[8,3712]{1,0:T(8,128)(2,1)S(1)} %pack.1.piece_ref), channel_id=1, source_target_pairs={{0,16},{2,18},{4,20},{6,22},{8,24},{10,26},{12,28},{14,30},{16,0},... | collective-permute-start | bytes 178184 | tf_op jit(solution)/shard_map/ppermute | solution.py:229
  7.3 1.9 %load_0.1 = (bf16[3584,1536]{1,0:T(8,128)(2,1)S(1)}, bf16[8,3712]{1,0:T(8,128)(2,1)S(1)}) custom-call(bf16[3584,1536]{1,0:T(8,128)(2,1)} %source.3, bf16[8,3712]{1,0:T(8,128)(2,1)S(1)} %pack.1.piece_ref), custom_call_target="tpu_custom_call" | custom-call | flops 805306368 | tf_op jit(solution)/shard_map/load_0/pallas_call | solution.py:97
  9.2 2.9 %collective-permute-done = bf16[8,3712]{1,0:T(8,128)(2,1)S(1)} collective-permute-done((bf16[8,3712]{1,0:T(8,128)(2,1)S(1)}, bf16[8,3712]{1,0:T(8,128)(2,1)S(1)}, u32[]{:S(2)}, u32[]{:S(2)}) %collective-permute-start) | collective-permute-done | bytes 59424 | tf_op jit(solution)/shard_map/ppermute | solution.py:229
  12.2 0.0 collective-permute-done.1
  12.2 0.0 collective-permute-done.2
  12.2 2.5 %collective-permute-start.8 = (bf16[32,3712]{1,0:T(8,128)(2,1)S(1)}, bf16[32,3712]{1,0:T(8,128)(2,1)S(1)}, u32[]{:S(2)}, u32[]{:S(2)}) collective-permute-start(bf16[32,3712]{1,0:T(8,128)(2,1)S(1)} %constant_dynamic-update-slice_fusion.piece_ref), channel_id=1, source_target_pairs={{0,6},{2,4},{4,2},{6,0},{8,14},{10,12},{12,10},{14,8},{16,22},{18,... | collective-permute-start | bytes 712712 | tf_op jit(solution)/shard_map/ppermute | solution.py:229
  14.7 0.5 %collective-permute-start.6 = (bf16[32,3712]{1,0:T(8,128)(2,1)S(1)}, bf16[32,3712]{1,0:T(8,128)(2,1)S(1)}, u32[]{:S(2)}, u32[]{:S(2)}) collective-permute-start(bf16[32,3712]{1,0:T(8,128)(2,1)S(1)} %constant_dynamic-update-slice_fusion.piece_ref), channel_id=1, source_target_pairs={{0,2},{2,0},{4,6},{6,4},{8,10},{10,8},{12,14},{14,12},{16,18},{18,... | collective-permute-start | bytes 712712 | tf_op jit(solution)/shard_map/ppermute | solution.py:229
  15.2 0.5 %collective-permute-start.4 = (bf16[32,3712]{1,0:T(8,128)(2,1)S(1)}, bf16[32,3712]{1,0:T(8,128)(2,1)S(1)}, u32[]{:S(2)}, u32[]{:S(2)}) collective-permute-start(bf16[32,3712]{1,0:T(8,128)(2,1)S(1)} %constant_dynamic-update-slice_fusion.piece_ref), channel_id=1, source_target_pairs={{0,4},{2,6},{4,0},{6,2},{8,12},{10,14},{12,8},{14,10},{16,20},{18,... | collective-permute-start | bytes 712712 | tf_op jit(solution)/shard_map/ppermute | solution.py:229
  15.8 3.3 %load_1024.1 = (bf16[3584,1536]{1,0:T(8,128)(2,1)S(1)}, bf16[32,3712]{1,0:T(8,128)(2,1)S(1)}) custom-call(bf16[3584,1536]{1,0:T(8,128)(2,1)} %source.3, bf16[32,3712]{1,0:T(8,128)(2,1)S(1)} %constant_dynamic-update-slice_fusion.piece_ref, bf16[3584,1536]{1,0:T(8,128)(2,1)S(1)} %get-tuple-element.9.refs_0_), custom_call_target="tpu_custom_call", output_to_operand_aliasing={{0}: (2, {})} | custom-call | flops 2013265920 | tf_op jit(solution)/shard_map/load_1024/pallas_call | solution.py:97
  19.1 0.1 collective-permute-start.3
  19.2 2.7 %collective-permute-done.8.refs_3_ = bf16[32,3712]{1,0:T(8,128)(2,1)S(1)} collective-permute-done((bf16[32,3712]{1,0:T(8,128)(2,1)S(1)}, bf16[32,3712]{1,0:T(8,128)(2,1)S(1)}, u32[]{:S(2)}, u32[]{:S(2)}) %collective-permute-start.8) | collective-permute-done | bytes 237600 | tf_op jit(solution)/shard_map/ppermute | solution.py:229
  21.8 0.0 collective-permute-start.9
  21.8 2.8 %collective-permute-done.6.refs_2_ = bf16[32,3712]{1,0:T(8,128)(2,1)S(1)} collective-permute-done((bf16[32,3712]{1,0:T(8,128)(2,1)S(1)}, bf16[32,3712]{1,0:T(8,128)(2,1)S(1)}, u32[]{:S(2)}, u32[]{:S(2)}) %collective-permute-start.6) | collective-permute-done | bytes 237600 | tf_op jit(solution)/shard_map/ppermute | solution.py:229
  24.7 0.0 collective-permute-start.7
  24.7 0.0 collective-permute-done.4.refs_1_
  24.7 0.5 %collective-permute-start.5 = (bf16[32,3712]{1,0:T(8,128)(2,1)S(1)}, bf16[32,3712]{1,0:T(8,128)(2,1)S(1)}, u32[]{:S(2)}, u32[]{:S(2)}) collective-permute-start(bf16[32,3712]{1,0:T(8,128)(2,1)S(1)} %collective-permute-done.4.refs_1_), channel_id=1, source_target_pairs={{0,1},{1,0},{2,3},{3,2},{4,5},{5,4},{6,7},{7,6},{8,9},{9,8},{10,11... | collective-permute-start | bytes 712712 | tf_op jit(solution)/shard_map/ppermute | solution.py:235
  25.2 2.0 %score_mine.1.refs_5_ = f32[2,128]{1,0:T(2,128)S(1)} custom-call(bf16[32,3712]{1,0:T(8,128)(2,1)S(1)} %get-tuple-element.10.refs_0_, bf16[32,3712]{1,0:T(8,128)(2,1)S(1)} %collective-permute-done.4.refs_1_, bf16[32,3712]{1,0:T(8,128)(2,1)S(1)} %collective-permute-done.6.refs_2_, bf16[32,3712]{1,0:T(8,128)(2,1)S(1)} %collective-permute-done.8.refs_3_, ...), custom_call_target="tpu_custom_call" | custom-call | flops 1409286144 | bytes 917504 | tf_op jit(solution)/shard_map/score_mine/pallas_call | solution.py:248
  27.2 0.0 collective-permute-done.3.refs_0_
  27.2 0.0 collective-permute-done.9.refs_3_
  27.2 0.0 collective-permute-done.7.refs_2_
  27.2 0.0 collective-permute-done.5.refs_1_
  27.3 2.1 %score_other.1 = f32[32,4,128]{2,1,0:T(4,128)S(1)} custom-call(bf16[32,3712]{1,0:T(8,128)(2,1)S(1)} %collective-permute-done.3.refs_0_, bf16[32,3712]{1,0:T(8,128)(2,1)S(1)} %collective-permute-done.5.refs_1_, bf16[32,3712]{1,0:T(8,128)(2,1)S(1)} %collective-permute-done.7.refs_2_, bf16[32,3712]{1,0:T(8,128)(2,1)S(1)} %collective-permute-done.9.refs_3_, ...), custom_call_target="tpu_custom_call" | custom-call | flops 1409286144 | bytes 917504 | tf_op jit(solution)/shard_map/score_other/pallas_call | solution.py:248
  29.4 10.7 %all_to_all.5.stats_ref = f32[32,4,128]{2,1,0:T(4,128)S(1)} all-to-all(f32[32,4,128]{2,1,0:T(4,128)S(1)} %score_other.1), channel_id=1, replica_groups=mesh['dp'=16,'vocab'=2] {'dp','vocab'}, dimensions={0} | all-to-all | bytes 131072 | tf_op jit(solution)/shard_map/all_to_all | solution.py:264
  40.0 0.7 %finish.1 = (f32[1,16]{1,0:T(1,128)}, f32[1,1]{1,0:T(1,128)}) custom-call(f32[32,4,128]{2,1,0:T(4,128)S(1)} %all_to_all.5.stats_ref), custom_call_target="tpu_custom_call" | custom-call | tf_op jit(solution)/shard_map/finish/pallas_call | solution.py:265
  (4 shorter events, 0.0 us)
Async XLA Ops:
  1.5 10.7 %collective-permute-start.2 = (bf16[8,3712]{1,0:T(8,128)(2,1)S(1)}, bf16[8,3712]{1,0:T(8,128)(2,1)S(1)}, u32[]{:S(2)}, u32[]{:S(2)}) collective-permute-start(bf16[8,3712]{1,0:T(8,128)(2,1)S(1)} %pack.1.piece_ref), channel_id=1, source_target_pairs={{0,24},{2,26},{4,28},{6,30},{8,16},{10,18},{12,20},{14,22},{16,8},... | collective-permute-start | bytes 178184 | tf_op jit(solution)/shard_map/ppermute | solution.py:229
  6.6 5.5 %collective-permute-start.1 = (bf16[8,3712]{1,0:T(8,128)(2,1)S(1)}, bf16[8,3712]{1,0:T(8,128)(2,1)S(1)}, u32[]{:S(2)}, u32[]{:S(2)}) collective-permute-start(bf16[8,3712]{1,0:T(8,128)(2,1)S(1)} %pack.1.piece_ref), channel_id=1, source_target_pairs={{0,8},{2,10},{4,12},{6,14},{8,0},{10,2},{12,4},{14,6},{16,24},{18,... | collective-permute-start | bytes 178184 | tf_op jit(solution)/shard_map/ppermute | solution.py:229
  6.6 5.5 %collective-permute-start = (bf16[8,3712]{1,0:T(8,128)(2,1)S(1)}, bf16[8,3712]{1,0:T(8,128)(2,1)S(1)}, u32[]{:S(2)}, u32[]{:S(2)}) collective-permute-start(bf16[8,3712]{1,0:T(8,128)(2,1)S(1)} %pack.1.piece_ref), channel_id=1, source_target_pairs={{0,16},{2,18},{4,20},{6,22},{8,24},{10,26},{12,28},{14,30},{16,0},... | collective-permute-start | bytes 178184 | tf_op jit(solution)/shard_map/ppermute | solution.py:229
  12.2 9.6 %collective-permute-start.8 = (bf16[32,3712]{1,0:T(8,128)(2,1)S(1)}, bf16[32,3712]{1,0:T(8,128)(2,1)S(1)}, u32[]{:S(2)}, u32[]{:S(2)}) collective-permute-start(bf16[32,3712]{1,0:T(8,128)(2,1)S(1)} %constant_dynamic-update-slice_fusion.piece_ref), channel_id=1, source_target_pairs={{0,6},{2,4},{4,2},{6,0},{8,14},{10,12},{12,10},{14,8},{16,22},{18,... | collective-permute-start | bytes 712712 | tf_op jit(solution)/shard_map/ppermute | solution.py:229
  14.7 10.0 %collective-permute-start.6 = (bf16[32,3712]{1,0:T(8,128)(2,1)S(1)}, bf16[32,3712]{1,0:T(8,128)(2,1)S(1)}, u32[]{:S(2)}, u32[]{:S(2)}) collective-permute-start(bf16[32,3712]{1,0:T(8,128)(2,1)S(1)} %constant_dynamic-update-slice_fusion.piece_ref), channel_id=1, source_target_pairs={{0,2},{2,0},{4,6},{6,4},{8,10},{10,8},{12,14},{14,12},{16,18},{18,... | collective-permute-start | bytes 712712 | tf_op jit(solution)/shard_map/ppermute | solution.py:229
  15.2 9.4 %collective-permute-start.4 = (bf16[32,3712]{1,0:T(8,128)(2,1)S(1)}, bf16[32,3712]{1,0:T(8,128)(2,1)S(1)}, u32[]{:S(2)}, u32[]{:S(2)}) collective-permute-start(bf16[32,3712]{1,0:T(8,128)(2,1)S(1)} %constant_dynamic-update-slice_fusion.piece_ref), channel_id=1, source_target_pairs={{0,4},{2,6},{4,0},{6,2},{8,12},{10,14},{12,8},{14,10},{16,20},{18,... | collective-permute-start | bytes 712712 | tf_op jit(solution)/shard_map/ppermute | solution.py:229
  19.1 8.1 %collective-permute-start.3 = (bf16[32,3712]{1,0:T(8,128)(2,1)S(1)}, bf16[32,3712]{1,0:T(8,128)(2,1)S(1)}, u32[]{:S(2)}, u32[]{:S(2)}) collective-permute-start(bf16[32,3712]{1,0:T(8,128)(2,1)S(1)} %get-tuple-element.10.refs_0_), channel_id=1, source_target_pairs={{0,1},{1,0},{2,3},{3,2},{4,5},{5,4},{6,7},{7,6},{8,9},{9,8},{10,11... | collective-permute-start | bytes 712712 | tf_op jit(solution)/shard_map/ppermute | solution.py:235
  21.8 5.4 %collective-permute-start.9 = (bf16[32,3712]{1,0:T(8,128)(2,1)S(1)}, bf16[32,3712]{1,0:T(8,128)(2,1)S(1)}, u32[]{:S(2)}, u32[]{:S(2)}) collective-permute-start(bf16[32,3712]{1,0:T(8,128)(2,1)S(1)} %collective-permute-done.8.refs_3_), channel_id=1, source_target_pairs={{0,1},{1,0},{2,3},{3,2},{4,5},{5,4},{6,7},{7,6},{8,9},{9,8},{10,11... | collective-permute-start | bytes 712712 | tf_op jit(solution)/shard_map/ppermute | solution.py:235
  24.7 2.6 %collective-permute-start.7 = (bf16[32,3712]{1,0:T(8,128)(2,1)S(1)}, bf16[32,3712]{1,0:T(8,128)(2,1)S(1)}, u32[]{:S(2)}, u32[]{:S(2)}) collective-permute-start(bf16[32,3712]{1,0:T(8,128)(2,1)S(1)} %collective-permute-done.6.refs_2_), channel_id=1, source_target_pairs={{0,1},{1,0},{2,3},{3,2},{4,5},{5,4},{6,7},{7,6},{8,9},{9,8},{10,11... | collective-permute-start | bytes 712712 | tf_op jit(solution)/shard_map/ppermute | solution.py:235
  24.7 2.6 %collective-permute-start.5 = (bf16[32,3712]{1,0:T(8,128)(2,1)S(1)}, bf16[32,3712]{1,0:T(8,128)(2,1)S(1)}, u32[]{:S(2)}, u32[]{:S(2)}) collective-permute-start(bf16[32,3712]{1,0:T(8,128)(2,1)S(1)} %collective-permute-done.4.refs_1_), channel_id=1, source_target_pairs={{0,1},{1,0},{2,3},{3,2},{4,5},{5,4},{6,7},{7,6},{8,9},{9,8},{10,11... | collective-permute-start | bytes 712712 | tf_op jit(solution)/shard_map/ppermute | solution.py:235
